TPU v7x, 32 devices: a whole 2x2x4 slice. The times are simulated.
32 devices in a mesh: row: 2 (over y), col: 16 (over z, x, core).
Axes of the slice: x: 2, y: 2, z: 4, core: 2. Of those that a mesh axis runs over, the one named last changes fastest.
Arguments:
- tokens: bfloat16 [512, 1024], P(('row', 'col')), may hold values from -6 to 6
- grad_out: bfloat16 [512, 1024], P(('row', 'col')), may hold values from -1.1953125 to 1.1953125
- gains: float32 [2, 1024], replicated, may hold values from 0.1 to 1.9
- flat_in: bfloat16 [16384, 2048], P(('row', 'col')), may hold values from -0.1875 to 0.1875
- flat_out: bfloat16 [16384, 2048], P(('row', 'col')), may hold values from -0.03125 to 0.03125
- flat_moment: float32 [2, 16384, 2048], P(None, ('row', 'col')), may hold values from -3 to 3
- flat_second: float32 [2, 16384, 2048], P(None, ('row', 'col')), may hold values from 0.05 to 2
- tile_in: bfloat16 [16, 6, 256, 2048], P('col', 'row'), may hold values from -0.1875 to 0.1875
- tile_out: bfloat16 [16, 6, 256, 2048], P('col', 'row'), may hold values from -0.03125 to 0.03125
- tile_moment: float32 [2, 16, 6, 256, 2048], P(None, 'col', 'row'), may hold values from -3 to 3
- tile_second: float32 [2, 16, 6, 256, 2048], P(None, 'col', 'row'), may hold values from 0.05 to 2
- owners: int32 [2, 16, 4], P(None, 'col'), may hold values from 0 to 1, as said below
Outputs:
- hidden_out: bfloat16 [512, 1024], P(('row', 'col'))
- grad_tokens: bfloat16 [512, 1024], P(('row', 'col'))
- new_flat_in: bfloat16 [16384, 2048], P(('row', 'col'))
- new_flat_out: bfloat16 [16384, 2048], P(('row', 'col'))
- new_flat_moment: float32 [2, 16384, 2048], P(None, ('row', 'col'))
- new_flat_second: float32 [2, 16384, 2048], P(None, ('row', 'col'))
- new_tile_in: bfloat16 [16, 6, 256, 2048], P('col', 'row')
- new_tile_out: bfloat16 [16, 6, 256, 2048], P('col', 'row')
- new_tile_moment: float32 [2, 16, 6, 256, 2048], P(None, 'col', 'row')
- new_tile_second: float32 [2, 16, 6, 256, 2048], P(None, 'col', 'row')
Inputs may be any that keep to these rules, and one draw needn't show every extreme that they name: `owners`: for each matrix and column block, entry k names the row that owns tile k; each row owns at most 3 tiles of a block and matrix, and in each block and matrix some row owns exactly 3.
All inputs are finite; a program needn't handle non-finite values.
Results may differ from a plain program's by a relative error of at most 0.029.
Values may be sent and summed in bfloat16 or wider, within the bound.
A program may use at most 192 MiB of HBM per device.

v0:
```python
import jax
import jax.numpy as jnp
from jax import lax
from jax.experimental import pallas as pl
from jax.experimental.pallas import tpu as pltpu
from jax.sharding import PartitionSpec as P

norm_eps = 1e-06
beta_one = 0.9
beta_two = 0.95
learn_rate = 0.002
decay_rate = 0.1
adam_eps = 1e-08
gelu_coef = 0.7978845608
both = ("row", "col")


def gelu_both(hidden):
    square = hidden * hidden
    tanh_term = jnp.tanh(gelu_coef * (hidden + 0.044715 * square * hidden))
    value = 0.5 * hidden * (1.0 + tanh_term)
    slope = 0.5 * (1.0 + tanh_term) + 0.5 * hidden * (1.0 - tanh_term * tanh_term) * gelu_coef * (
        1.0 + 0.134145 * square
    )
    return value, slope


def adam_update(weight, gradient, moment, second):
    new_moment = beta_one * moment + (1.0 - beta_one) * gradient
    new_second = beta_two * second + (1.0 - beta_two) * gradient * gradient
    weight_float = weight.astype(jnp.float32)
    stepped = weight_float - learn_rate * (
        new_moment / (jnp.sqrt(new_second) + adam_eps) + decay_rate * weight_float
    )
    return (stepped.astype(jnp.bfloat16), new_moment, new_second)


def tile_ranks(owner_rows):
    positions = jnp.arange(owner_rows.shape[-1], dtype=jnp.int32)
    same_owner = owner_rows[..., :, None] == owner_rows[..., None, :]
    earlier = positions[None, :] < positions[:, None]
    return jnp.sum(jnp.where(same_owner & earlier, 1, 0), axis=-1).astype(jnp.int32)


def flat_kernel(w_in, w_out, g_in, g_out, mom, sec, o_in, o_out, o_mom, o_sec):
    for m, (w, g, o) in enumerate(((w_in, g_in, o_in), (w_out, g_out, o_out))):
        new = adam_update(w[...], g[...].astype(jnp.float32), mom[m], sec[m])
        o[...], o_mom[m], o_sec[m] = new


def flat_adam(w_in, w_out, g_in, g_out, mom, sec):
    rows, width = w_in.shape
    step = min(rows, 32)
    thin = pl.BlockSpec((step, width), lambda i: (i, 0))
    wide = pl.BlockSpec((2, step, width), lambda i: (0, i, 0))
    shape = jax.ShapeDtypeStruct
    return pl.pallas_call(
        flat_kernel,
        grid=(rows // step,),
        in_specs=[thin, thin, thin, thin, wide, wide],
        out_specs=[thin, thin, wide, wide],
        out_shape=[
            shape(w_in.shape, w_in.dtype),
            shape(w_out.shape, w_out.dtype),
            shape(mom.shape, mom.dtype),
            shape(sec.shape, sec.dtype),
        ],
        cost_estimate=pl.CostEstimate(
            flops=30 * mom.size, bytes_accessed=20 * mom.size + 2 * mom.size, transcendentals=mom.size
        ),
        name="flat_adam",
    )(w_in, w_out, g_in, g_out, mom, sec)


def tile_kernel(
    tiles, live, me, l_in, l_out, r_in, r_out, w_in, w_out, mom, sec, o_in, o_out, o_mom, o_sec
):
    slot = pl.program_id(0)
    parts = ((l_in, r_in, w_in, o_in), (l_out, r_out, w_out, o_out))
    for m, (left, right, w, o) in enumerate(parts):
        grad = jnp.dot(left[...], right[0], preferred_element_type=jnp.float32)
        alive = live[m, slot] > 0
        old_w, old_m, old_s = w[0, 0], mom[m, 0, 0], sec[m, 0, 0]
        new_w, new_m, new_s = adam_update(old_w, grad, old_m, old_s)
        o[0, 0] = jnp.where(alive, new_w.astype(jnp.float32), old_w.astype(jnp.float32)).astype(
            jnp.bfloat16
        )
        o_mom[m, 0, 0] = jnp.where(alive, new_m, old_m)
        o_sec[m, 0, 0] = jnp.where(alive, new_s, old_s)


def tile_adam(tiles, live, me, l_in, l_out, r_in, r_out, w_in, w_out, mom, sec):
    slot_cap, tile_rows, width = w_in.shape[1:]
    ranks, toks, sub = r_in.shape
    step = min(sub, 512)
    per = sub // step

    def left_map(m):
        return lambda s, h, tiles, live, me: (tiles[m, s], 0)

    def right_map(s, h, tiles, live, me):
        return (lax.rem(me[0] + ranks - h // per, ranks), 0, h % per)

    def thin_map(s, h, *unused):
        return (0, s, 0, h)

    def wide_map(s, h, *unused):
        return (0, 0, s, 0, h)

    right = pl.BlockSpec((1, toks, step), right_map)
    thin = pl.BlockSpec((1, 1, tile_rows, step), thin_map)
    wide = pl.BlockSpec((2, 1, 1, tile_rows, step), wide_map)
    shape = jax.ShapeDtypeStruct
    return pl.pallas_call(
        tile_kernel,
        grid_spec=pltpu.PrefetchScalarGridSpec(
            num_scalar_prefetch=3,
            grid=(slot_cap, width // step),
            in_specs=[
                pl.BlockSpec((tile_rows, toks), left_map(0)),
                pl.BlockSpec((tile_rows, toks), left_map(1)),
                right,
                right,
                thin,
                thin,
                wide,
                wide,
            ],
            out_specs=[thin, thin, wide, wide],
        ),
        out_shape=[
            shape(w_in.shape, w_in.dtype),
            shape(w_out.shape, w_out.dtype),
            shape(mom.shape, mom.dtype),
            shape(sec.shape, sec.dtype),
        ],
        cost_estimate=pl.CostEstimate(
            flops=2 * toks * mom.size, bytes_accessed=22 * mom.size, transcendentals=mom.size
        ),
        name="tile_adam",
    )(tiles, live, me, l_in, l_out, r_in, r_out, w_in, w_out, mom, sec)


def row_swap(pieces_for, row_total):
    got = [pieces_for(0)]
    for shift in range(1, row_total):
        pairs = [(src, (src + shift) % row_total) for src in range(row_total)]
        got.append(lax.ppermute(pieces_for(shift), "row", pairs))
    return jnp.stack(got)


def spread_sum(partial, total):
    toks, width = partial.shape
    sent = partial.astype(jnp.bfloat16)
    came = lax.all_to_all(sent, both, split_axis=0, concat_axis=0, tiled=True)
    return jnp.sum(came.reshape(total, toks // total, width).astype(jnp.float32), axis=0)


def late_sum(partial):
    return lax.psum_scatter(
        partial.astype(jnp.bfloat16), both, scatter_dimension=0, tiled=True
    ).astype(jnp.float32)


def dot_nt(left, right):
    return lax.dot_general(left, right, (((1,), (1,)), ((), ())), preferred_element_type=jnp.float32)


def dot_tn(left, right):
    return lax.dot_general(left, right, (((0,), (0,)), ((), ())), preferred_element_type=jnp.float32)


def norm_of(layer_in, gain_vec):
    tok_float = layer_in.astype(jnp.float32)
    inv_rms = lax.rsqrt(jnp.mean(tok_float * tok_float, axis=1, keepdims=True) + norm_eps)
    normed = (tok_float * inv_rms * gain_vec).astype(jnp.bfloat16)
    return tok_float, inv_rms, normed


def token_grad(cotangent, d_normed, gain_vec, tok_float, inv_rms):
    gated = d_normed * gain_vec
    return (
        cotangent.astype(jnp.float32)
        + inv_rms * gated
        - tok_float
        * inv_rms
        * inv_rms
        * inv_rms
        * jnp.mean(tok_float * gated, axis=1, keepdims=True)
    ).astype(jnp.bfloat16)


def shards(
    tokens,
    grad_out,
    gains,
    flat_in,
    flat_out,
    flat_moment,
    flat_second,
    tile_in,
    tile_out,
    tile_moment,
    tile_second,
    owners,
):
    row_total = lax.axis_size("row")
    col_total = lax.axis_size("col")
    total = row_total * col_total
    row_index = lax.axis_index("row")
    model_width = tokens.shape[1]
    block = flat_in.shape[1]
    sub = block // row_total
    own_rows = flat_in.shape[0] // col_total
    slot_cap = tile_in.shape[1]
    tile_rows = tile_in.shape[2]

    owner_rows = owners[:, 0, :]
    ranks = tile_ranks(owner_rows)
    came_from = lax.rem(row_index - owner_rows + row_total, row_total)
    slot_pick = came_from * slot_cap + ranks
    slots = jnp.arange(slot_cap, dtype=jnp.int32)[None, :, None]
    mine = (owner_rows == row_index)[:, None, :] & (ranks[:, None, :] == slots)
    positions = jnp.arange(owner_rows.shape[1], dtype=jnp.int32)
    my_tiles = jnp.sum(jnp.where(mine, positions, 0), axis=-1).astype(jnp.int32)
    my_live = jnp.any(mine, axis=-1).astype(jnp.int32)

    def flat_to_units(flat):
        parts = flat.reshape(own_rows, col_total, row_total, sub).transpose(2, 1, 0, 3)
        return lax.all_to_all(
            parts.reshape(total * own_rows, sub), both, split_axis=0, concat_axis=0, tiled=True
        )

    def units_to_flat(grad):
        came = lax.all_to_all(
            grad.astype(jnp.bfloat16), both, split_axis=0, concat_axis=0, tiled=True
        )
        parts = came.reshape(row_total, col_total, own_rows, sub).transpose(2, 1, 0, 3)
        return parts.reshape(own_rows * col_total, block)

    def tiles_to_units(tile, pick):
        def piece(shift):
            to_row = lax.rem(row_index + shift, row_total)
            return lax.dynamic_slice_in_dim(tile[0], to_row * sub, sub, 2)

        whole = row_swap(piece, row_total).reshape(row_total * slot_cap, tile_rows, sub)
        return jnp.take(whole, pick, axis=0).reshape(model_width, sub)

    def gather(x):
        return lax.all_gather(x, both, axis=0, tiled=True)

    tok_one, inv_one, normed_one = norm_of(tokens, gains[0])
    normed_one = gather(normed_one)
    one_in = flat_to_units(flat_in)
    one_out = flat_to_units(flat_out)
    cot_two = gather(grad_out)
    two_in = tiles_to_units(tile_in, slot_pick[0])
    two_out = tiles_to_units(tile_out, slot_pick[1])
    hidden_one = jnp.dot(normed_one, one_in, preferred_element_type=jnp.float32)
    act_one, slope_one = gelu_both(hidden_one)
    act_one = act_one.astype(jnp.bfloat16)
    middle = (tok_one + spread_sum(dot_nt(act_one, one_out), total)).astype(jnp.bfloat16)

    tok_two, inv_two, normed_two = norm_of(middle, gains[1])
    normed_two = gather(normed_two)
    hidden_two = jnp.dot(normed_two, two_in, preferred_element_type=jnp.float32)
    act_two, slope_two = gelu_both(hidden_two)
    act_two = act_two.astype(jnp.bfloat16)
    d_act_two = jnp.dot(cot_two, two_out, preferred_element_type=jnp.float32)
    d_hidden_two = (d_act_two * slope_two).astype(jnp.bfloat16)
    d_normed_two = spread_sum(dot_nt(d_hidden_two, two_in), total)
    grad_mid = token_grad(grad_out, d_normed_two, gains[1], tok_two, inv_two)
    cot_one = gather(grad_mid)

    d_act_one = jnp.dot(cot_one, one_out, preferred_element_type=jnp.float32)
    d_hidden_one = (d_act_one * slope_one).astype(jnp.bfloat16)
    flat_grad_in = units_to_flat(dot_tn(normed_one, d_hidden_one))
    flat_grad_out = units_to_flat(dot_tn(cot_one, act_one))

    act_late, _ = lax.optimization_barrier((act_two, cot_one))
    mixed_two = late_sum(dot_nt(act_late, two_out))
    hidden_out = (tok_two + mixed_two).astype(jnp.bfloat16)
    d_normed_one = late_sum(dot_nt(d_hidden_one, one_in))
    grad_tokens = token_grad(grad_mid, d_normed_one, gains[0], tok_one, inv_one)

    d_hidden_rows = row_swap(lambda shift: d_hidden_two, row_total)
    act_rows = row_swap(lambda shift: act_two, row_total)
    new_tile = tile_adam(
        my_tiles,
        my_live,
        row_index.astype(jnp.int32).reshape(1),
        normed_two.T,
        cot_two.T,
        d_hidden_rows,
        act_rows,
        tile_in,
        tile_out,
        tile_moment,
        tile_second,
    )
    new_flat = flat_adam(flat_in, flat_out, flat_grad_in, flat_grad_out, flat_moment, flat_second)
    return (hidden_out, grad_tokens, *new_flat, *new_tile)


def solution(mesh):
    return jax.shard_map(
        shards,
        mesh=mesh,
        in_specs=(
            P(("row", "col"), None),
            P(("row", "col"), None),
            P(),
            P(("row", "col"), None),
            P(("row", "col"), None),
            P(None, ("row", "col"), None),
            P(None, ("row", "col"), None),
            P("col", "row", None, None),
            P("col", "row", None, None),
            P(None, "col", "row", None, None),
            P(None, "col", "row", None, None),
            P(None, "col", None),
        ),
        out_specs=(
            P(("row", "col"), None),
            P(("row", "col"), None),
            P(("row", "col"), None),
            P(("row", "col"), None),
            P(None, ("row", "col"), None),
            P(None, ("row", "col"), None),
            P("col", "row", None, None),
            P("col", "row", None, None),
            P(None, "col", "row", None, None),
            P(None, "col", "row", None, None),
        ),
        check_vma=False,
    )
```

profile of v0, /device:TPU:0, one launch (start us, length us, event | category | flops | bytes accessed | tf_op | source)
XLA Modules:
  0.0 712.5 jit_solution(11451729788757894904)
XLA Ops:
  7.2 3.3 reshape.124
  10.5 2.5 copy.63
  13.0 7.5 %all-to-all-start = ((bf16[32,32,1024]{2,1,0:T(8,128)(2,1)}), bf16[32,32,1024]{2,1,0:T(8,128)(2,1)}, u32[]{:S(2)}, u32[]{:S(2)}) async-start(bf16[32,32,1024]{2,1,0:T(8,128)(2,1)} %bitcast.80), calls=%async_computation | async-start | bytes 4194304 | tf_op jit(solution)/shard_map/all_to_all | solution.py:230
  20.4 2.8 reshape.125
  23.2 4.1 copy.64
  27.2 42.8 %all-to-all-done = bf16[32,32,1024]{2,1,0:T(8,128)(2,1)} async-done(((bf16[32,32,1024]{2,1,0:T(8,128)(2,1)}), bf16[32,32,1024]{2,1,0:T(8,128)(2,1)}, u32[]{:S(2)}, u32[]{:S(2)}) %all-to-all-start) | async-done | bytes 2097184 | tf_op jit(solution)/shard_map/all_to_all | solution.py:230
  70.1 2.9 all-to-all-start.1
  73.9 64.5 %all-gather.5.cloned.1.call-done = bf16[512,1024]{1,0:T(8,128)(2,1)} async-done(((bf16[16,1024]{1,0:T(8,128)(2,1)}), bf16[512,1024]{1,0:T(8,128)(2,1)}) %all-gather.5.cloned.1.call-update) | async-done | bytes 1048592 | tf_op jit(solution)/shard_map/all_gather | solution.py:250
  138.5 4.5 fusion.32
  144.3 3.0 convolution_convert_fusion.5
  147.3 30.6 %all_to_all.60 = bf16[32,16,1024]{2,1,0:T(8,128)(2,1)S(1)} all-to-all(bf16[32,16,1024]{2,1,0:T(8,128)(2,1)S(1)} %bitcast.97), channel_id=1, replica_groups=mesh['row'=2,'col'=16] {'row','col'}, dimensions={0} | all-to-all | bytes 2097152 | tf_op jit(solution)/shard_map/all_to_all | solution.py:155
  179.0 2.1 constant_dynamic-slice_fusion.1
  182.0 2.0 constant_dynamic-slice_fusion
  185.6 34.0 %collective-permute-done = bf16[3,256,1024]{2,1,0:T(8,128)(2,1)S(1)} collective-permute-done((bf16[3,256,1024]{2,1,0:T(8,128)(2,1)}, bf16[3,256,1024]{2,1,0:T(8,128)(2,1)S(1)}, u32[]{:S(2)}, u32[]{:S(2)}) %collective-permute-start) | collective-permute-done | bytes 1572896 | tf_op jit(solution)/shard_map/ppermute | solution.py:148
  220.8 2.2 pad_maximum_fusion
  223.0 2.0 gather_fusion
  225.0 28.6 %collective-permute-done.1 = bf16[3,256,1024]{2,1,0:T(8,128)(2,1)} collective-permute-done((bf16[3,256,1024]{2,1,0:T(8,128)(2,1)}, bf16[3,256,1024]{2,1,0:T(8,128)(2,1)}, u32[]{:S(2)}, u32[]{:S(2)}) %collective-permute-start.1) | collective-permute-done | bytes 1572896 | tf_op jit(solution)/shard_map/ppermute | solution.py:148
  253.6 2.2 pad_maximum_fusion.1
  255.8 2.0 gather_fusion.1
  257.8 4.0 broadcast_select_fusion
  261.7 5.5 multiply_convert_fusion.1
  267.3 19.5 %all-gather.9.cloned.1.call-done = bf16[512,1024]{1,0:T(8,128)(2,1)} async-done(((bf16[16,1024]{1,0:T(8,128)(2,1)}), bf16[512,1024]{1,0:T(8,128)(2,1)}) %all-gather.9.cloned.1.call-update) | async-done | bytes 1048592 | tf_op jit(solution)/shard_map/all_gather | solution.py:250
  286.8 4.2 fusion.4
  292.3 30.6 %all_to_all.61 = bf16[32,16,1024]{2,1,0:T(8,128)(2,1)S(1)} all-to-all(bf16[32,16,1024]{2,1,0:T(8,128)(2,1)S(1)} %bitcast.96), channel_id=1, replica_groups=mesh['row'=2,'col'=16] {'row','col'}, dimensions={0} | all-to-all | bytes 2097152 | tf_op jit(solution)/shard_map/all_to_all | solution.py:155
  323.9 51.1 %all-gather.11.cloned.1.call-done = bf16[512,1024]{1,0:T(8,128)(2,1)} async-done(((bf16[16,1024]{1,0:T(8,128)(2,1)}), bf16[512,1024]{1,0:T(8,128)(2,1)}) %all-gather.11.cloned.1.call-update) | async-done | bytes 1048592 | tf_op jit(solution)/shard_map/all_gather | solution.py:250
  375.0 4.0 convolution_convert_fusion
  379.0 3.6 all-to-all-start.5
  382.6 4.6 multiply_convert_fusion
  388.2 3.9 convolution_convert_fusion.2
  392.1 4.2 convolution_convert_fusion.1
  396.3 37.6 %all-to-all-done.5 = bf16[32,32,1024]{2,1,0:T(8,128)(2,1)S(1)} async-done(((bf16[32,32,1024]{2,1,0:T(8,128)(2,1)}), bf16[32,32,1024]{2,1,0:T(8,128)(2,1)S(1)}, u32[]{:S(2)}, u32[]{:S(2)}) %all-to-all-start.5) | async-done | bytes 2097184 | tf_op jit(solution)/shard_map/all_to_all | solution.py:235
  433.9 3.5 all-to-all-start.4
  437.7 3.8 convolution_convert_fusion.3
  441.5 1.6 collective-permute-start.2
  445.1 2.3 copy.74
  448.7 37.4 %collective-permute-done.2 = bf16[512,1024]{1,0:T(8,128)(2,1)} collective-permute-done((bf16[512,1024]{1,0:T(8,128)(2,1)}, bf16[512,1024]{1,0:T(8,128)(2,1)}, u32[]{:S(2)}, u32[]{:S(2)}) %collective-permute-start.2) | collective-permute-done | bytes 1048608 | tf_op jit(solution)/shard_map/ppermute | solution.py:148
  486.1 3.1 pad_maximum_fusion.2.r_in
  489.2 21.3 %collective-permute-done.3 = bf16[512,1024]{1,0:T(8,128)(2,1)} collective-permute-done((bf16[512,1024]{1,0:T(8,128)(2,1)}, bf16[512,1024]{1,0:T(8,128)(2,1)}, u32[]{:S(2)}, u32[]{:S(2)}) %collective-permute-start.3) | collective-permute-done | bytes 1048608 | tf_op jit(solution)/shard_map/ppermute | solution.py:148
  510.5 2.7 pad_maximum_fusion.3.r_out
  513.2 31.7 %tile_adam.1 = (bf16[1,3,256,2048]{3,2,1,0:T(8,128)(2,1)}, bf16[1,3,256,2048]{3,2,1,0:T(8,128)(2,1)}, f32[2,1,3,256,2048]{4,3,2,1,0:T(8,128)}, f32[2,1,3,256,2048]{4,3,2,1,0:T(8,128)}) custom-call(s32[2,3]{1,0:T(2,128)} %select_reduce_fusion.tiles, s32[2,3]{1,0:T(2,128)} %convert_element_type.99.live, s32[1]{0:T(128)} %bitcast.28.me, ...), custom_call_target="tpu_custom_call" | custom-call | flops 3221225472 | bytes 69206016 | tf_op jit(solution)/shard_map/tile_adam/pallas_call | solution.py:114
  545.8 124.0 %reduce-scatter.7.cloned.1.call-done = bf16[16,1024]{1,0:T(8,128)(2,1)} async-done(((bf16[512,1024]{1,0:T(8,128)(2,1)}), bf16[16,1024]{1,0:T(8,128)(2,1)}) %reduce-scatter.7.cloned.1.call-update) | async-done | bytes 32784 | tf_op jit(solution)/shard_map/reduce_scatter | solution.py:160
  669.8 1.4 fusion.24
  671.2 1.5 fusion.18
  672.7 2.2 copy.71
  674.8 1.9 copy.84
  676.8 3.7 copy.70
  680.5 2.0 copy.83
  682.5 23.2 %flat_adam.1 = (bf16[512,2048]{1,0:T(8,128)(2,1)}, bf16[512,2048]{1,0:T(8,128)(2,1)}, f32[2,512,2048]{2,1,0:T(8,128)}, f32[2,512,2048]{2,1,0:T(8,128)}) custom-call(bf16[512,2048]{1,0:T(8,128)(2,1)} %w_in.2, bf16[512,2048]{1,0:T(8,128)(2,1)} %w_out.2, bf16[512,2048]{1,0:T(8,128)(2,1)} %bitcast.78, bf16[512,2048]{1,0:T(8,128)(2,1)} %bitcast.77, ...), custom_call_target="tpu_custom_call" | custom-call | flops 62914560 | bytes 46137344 | tf_op jit(solution)/shard_map/flat_adam/pallas_call | solution.py:57
  (82 shorter events, 14.7 us)
Async XLA Ops:
  13.0 7.5 %copy-start.2 = (bf16[512,2048]{1,0:T(8,128)(2,1)S(1)}, bf16[512,2048]{1,0:T(8,128)(2,1)}, u32[]{:S(2)}) copy-start(bf16[512,2048]{1,0:T(8,128)(2,1)} %w_out.2) | copy-start | bytes 6291460
  13.0 57.1 %all-to-all-start = ((bf16[32,32,1024]{2,1,0:T(8,128)(2,1)}), bf16[32,32,1024]{2,1,0:T(8,128)(2,1)}, u32[]{:S(2)}, u32[]{:S(2)}) async-start(bf16[32,32,1024]{2,1,0:T(8,128)(2,1)} %bitcast.80), calls=%async_computation | async-start | bytes 4194304 | tf_op jit(solution)/shard_map/all_to_all | solution.py:230
  70.1 2.9 copy-start.11
  70.1 3.1 copy-start.15
  70.1 72.9 %all-to-all-start.1 = ((bf16[32,32,1024]{2,1,0:T(8,128)(2,1)}), bf16[32,32,1024]{2,1,0:T(8,128)(2,1)S(1)}, u32[]{:S(2)}, u32[]{:S(2)}) async-start(bf16[32,32,1024]{2,1,0:T(8,128)(2,1)} %bitcast.5), calls=%async_computation.1 | async-start | bytes 4194304 | tf_op jit(solution)/shard_map/all_to_all | solution.py:230
  73.0 65.5 %all-gather.5.cloned.1.call-start = ((), (), s32[]{:S(2)}) async-start(), calls=%async_computation.8 | async-start | bytes 1081344 | tf_op jit(solution)/shard_map/all_gather | solution.py:250
  73.9 187.9 %all-gather.7.cloned.1.call-start = ((), (), s32[]{:S(2)}) async-start(), calls=%async_computation.9 | async-start | bytes 1081344 | tf_op jit(solution)/shard_map/all_gather | solution.py:250
  143.0 1.3 copy-start.5
  147.3 31.7 %copy-start.1 = (bf16[1,3,256,2048]{3,2,1,0:T(8,128)(2,1)S(1)}, bf16[1,3,256,2048]{3,2,1,0:T(8,128)(2,1)}, u32[]{:S(2)}) copy-start(bf16[1,3,256,2048]{3,2,1,0:T(8,128)(2,1)} %w_in.3) | copy-start | bytes 9437188
  178.9 107.9 %all-gather.9.cloned.1.call-start = ((), (), s32[]{:S(2)}) async-start(), calls=%async_computation.10 | async-start | bytes 1081344 | tf_op jit(solution)/shard_map/all_gather | solution.py:250
  179.0 3.0 copy-start
  181.1 4.3 copy-start.14
  181.1 38.6 %collective-permute-start = (bf16[3,256,1024]{2,1,0:T(8,128)(2,1)}, bf16[3,256,1024]{2,1,0:T(8,128)(2,1)S(1)}, u32[]{:S(2)}, u32[]{:S(2)}) collective-permute-start(bf16[3,256,1024]{2,1,0:T(8,128)(2,1)} %get-tuple-element.68), channel_id=1, source_target_pairs={{0,16},{16,0},{1,17},{17,1},{2,18},{18,2},{3,19},{19,3},{4,20},{20... | collective-permute-start | bytes 4718600 | tf_op jit(solution)/shard_map/ppermute | solution.py:148
  184.0 69.6 %collective-permute-start.1 = (bf16[3,256,1024]{2,1,0:T(8,128)(2,1)}, bf16[3,256,1024]{2,1,0:T(8,128)(2,1)}, u32[]{:S(2)}, u32[]{:S(2)}) collective-permute-start(bf16[3,256,1024]{2,1,0:T(8,128)(2,1)} %get-tuple-element.66), channel_id=1, source_target_pairs={{0,16},{16,0},{1,17},{17,1},{2,18},{18,2},{3,19},{19,3},{4,20},{20... | collective-permute-start | bytes 4718600 | tf_op jit(solution)/shard_map/ppermute | solution.py:148
  185.1 189.9 %all-gather.11.cloned.1.call-start = ((), (), s32[]{:S(2)}) async-start(), calls=%async_computation.11 | async-start | bytes 1081344 | tf_op jit(solution)/shard_map/all_gather | solution.py:250
  219.7 1.1 copy-start.6
  261.7 25.1 %copy-start.3 = (bf16[4,256,1024]{2,1,0:T(8,128)(2,1)}, bf16[4,256,1024]{2,1,0:T(8,128)(2,1)S(1)}, u32[]{:S(2)}) copy-start(bf16[4,256,1024]{2,1,0:T(8,128)(2,1)S(1)} %get-tuple-element.75) | copy-start | bytes 6291460
  267.3 170.4 %copy-start.8 = (bf16[512,1024]{1,0:T(8,128)(2,1)}, bf16[512,1024]{1,0:T(8,128)(2,1)S(1)}, u32[]{:S(2)}) copy-start(bf16[512,1024]{1,0:T(8,128)(2,1)S(1)} %get-tuple-element.20) | copy-start | bytes 3145732
  286.8 4.2 copy-start.4
  291.0 1.3 copy-start.10
  292.3 30.9 %copy-start.13 = (bf16[16,1024]{1,0:T(8,128)(2,1)S(1)}, bf16[16,1024]{1,0:T(8,128)(2,1)}, u32[]{:S(2)}) copy-start(bf16[16,1024]{1,0:T(8,128)(2,1)} %param.15) | copy-start | bytes 98308
  292.3 82.7 %copy-start.16 = (f32[512,1024]{1,0:T(8,128)S(1)}, f32[512,1024]{1,0:T(8,128)}, u32[]{:S(2)}) copy-start(f32[512,1024]{1,0:T(8,128)} %fusion.32) | copy-start | bytes 6291460
  379.0 54.9 %all-to-all-start.5 = ((bf16[32,32,1024]{2,1,0:T(8,128)(2,1)}), bf16[32,32,1024]{2,1,0:T(8,128)(2,1)S(1)}, u32[]{:S(2)}, u32[]{:S(2)}) async-start(bf16[32,32,1024]{2,1,0:T(8,128)(2,1)} %bitcast.94), calls=%async_computation.5 | async-start | bytes 4194304 | tf_op jit(solution)/shard_map/all_to_all | solution.py:235
  382.6 162.4 %reduce-scatter.9.cloned.1.call-start = ((), (), s32[]{:S(2)}) async-start(), calls=%async_computation.13 | async-start | bytes 1081344 | tf_op jit(solution)/shard_map/reduce_scatter | solution.py:160
  387.3 1.0 copy-start.17
  433.9 242.9 %all-to-all-start.4 = ((bf16[32,32,1024]{2,1,0:T(8,128)(2,1)}), bf16[32,32,1024]{2,1,0:T(8,128)(2,1)}, u32[]{:S(2)}, u32[]{:S(2)}) async-start(bf16[32,32,1024]{2,1,0:T(8,128)(2,1)} %bitcast.93), calls=%async_computation.4 | async-start | bytes 4194304 | tf_op jit(solution)/shard_map/all_to_all | solution.py:235
  437.4 232.5 %reduce-scatter.7.cloned.1.call-start = ((), (), s32[]{:S(2)}) async-start(), calls=%async_computation.12 | async-start | bytes 1081344 | tf_op jit(solution)/shard_map/reduce_scatter | solution.py:160
  441.5 5.8 copy-start.7
  441.5 44.6 %collective-permute-start.2 = (bf16[512,1024]{1,0:T(8,128)(2,1)}, bf16[512,1024]{1,0:T(8,128)(2,1)}, u32[]{:S(2)}, u32[]{:S(2)}) collective-permute-start(bf16[512,1024]{1,0:T(8,128)(2,1)} %copy-done.10), channel_id=1, source_target_pairs={{0,16},{16,0},{1,17},{17,1},{2,18},{18,2},{3,19},{19,3},{4,20},{20... | collective-permute-start | bytes 3145736 | tf_op jit(solution)/shard_map/ppermute | solution.py:148
  443.2 67.3 %collective-permute-start.3 = (bf16[512,1024]{1,0:T(8,128)(2,1)}, bf16[512,1024]{1,0:T(8,128)(2,1)}, u32[]{:S(2)}, u32[]{:S(2)}) collective-permute-start(bf16[512,1024]{1,0:T(8,128)(2,1)} %copy-done.8), channel_id=1, source_target_pairs={{0,16},{16,0},{1,17},{17,1},{2,18},{18,2},{3,19},{19,3},{4,20},{20... | collective-permute-start | bytes 3145736 | tf_op jit(solution)/shard_map/ppermute | solution.py:148
  486.1 24.4 %copy-start.9 = (bf16[512,1024]{1,0:T(8,128)(2,1)S(1)}, bf16[512,1024]{1,0:T(8,128)(2,1)}, u32[]{:S(2)}) copy-start(bf16[512,1024]{1,0:T(8,128)(2,1)} %copy-done.8) | copy-start | bytes 3145732
  513.2 158.0 %copy-start.12 = (bf16[16,1024]{1,0:T(8,128)(2,1)S(1)}, bf16[16,1024]{1,0:T(8,128)(2,1)}, u32[]{:S(2)}) copy-start(bf16[16,1024]{1,0:T(8,128)(2,1)} %fusion.13) | copy-start | bytes 98308
Sparse Core Ops, SparseCore 0:
  77.2 61.2 all-gather.4
  179.0 52.1 all-gather.6
  234.1 52.6 all-gather.8
  324.0 50.9 all-gather.10
  392.2 141.6 reduce-scatter.8
  536.6 133.1 reduce-scatter.6
where the time goes:
time: 714 us; the launch traced here: 712 us
  waiting for transfers between devices  461 us (65%)
  blocking collectives  61.1 us (9%)
  Pallas kernels  54.9 us (8%)
  matrix products  39 us (5%)
  local copies, waits for them, and re-layouts  37.6 us (5%)
  other arithmetic  22.4 us (3%)
  starting transfers between devices  22.1 us (3%)
  between operations  14.4 us (2%)
    all_gather x4, waiting for transfers between devices, gather(): return lax.all_gather(x, both, axis=0, tiled=True)  135 us
    reduce_scatter x2, waiting for transfers between devices, late_sum(): lax.psum_scatter(partial.astype(jnp.bfloat16), both, scatter_dimension=0,...  124 us
    ppermute x4, waiting for transfers between devices, row_swap(): got.append(lax.ppermute(pieces_for(shift), 'row', pairs))  121 us
    all_to_all x2, blocking collectives, spread_sum(): came = lax.all_to_all(sent, both, split_axis=0, concat_axis=0, tiled=True)  61.1 us
    all_to_all x2, waiting for transfers between devices, flat_to_units(): lax.all_to_all(parts.reshape(total * own_rows, sub), both, split_axis=0,...  42.8 us
    all_to_all x2, waiting for transfers between devices, units_to_flat(): lax.all_to_all(grad.astype(jnp.bfloat16), both, split_axis=0, concat_axis...  37.6 us
    pallas_call x1, Pallas kernels, tile_adam(): pl.pallas_call(tile_kernel, grid_spec=pltpu.PrefetchScalarGridSpec(num_sc...  31.7 us
    pallas_call x1, Pallas kernels, flat_adam(): pl.pallas_call(flat_kernel, grid=(rows // step,), in_specs=[thin, thin, t...  23.2 us
  transfers between devices with their start and end apart: 14, of which 10 were waited for; matrix products, arithmetic and copies ran while one was open for 10% of the time, Pallas kernels for 4%

commit v1 on v0

--- a/solution.py
+++ b/solution.py
@@ -1,3 +1,5 @@
+import functools
+
 import jax
 import jax.numpy as jnp
 from jax import lax
@@ -206,6 +208,23 @@
 ):
     row_total = lax.axis_size("row")
     col_total = lax.axis_size("col")
+    dims = fused_dims(row_total, col_total, tokens, flat_in, tile_in, owners)
+    if dims is not None:
+        return fused_shards(
+            dims,
+            tokens,
+            grad_out,
+            gains,
+            flat_in,
+            flat_out,
+            flat_moment,
+            flat_second,
+            tile_in,
+            tile_out,
+            tile_moment,
+            tile_second,
+            owners,
+        )
     total = row_total * col_total
     row_index = lax.axis_index("row")
     model_width = tokens.shape[1]
@@ -300,6 +319,761 @@
     )
     new_flat = flat_adam(flat_in, flat_out, flat_grad_in, flat_grad_out, flat_moment, flat_second)
     return (hidden_out, grad_tokens, *new_flat, *new_tile)
+
+
+MESH = pl.DeviceIdType.MESH
+
+
+def middle_kernel(
+    dims,
+    pick,
+    tok_ref,
+    gout_ref,
+    gains_ref,
+    flat_in,
+    flat_out,
+    tile_in,
+    tile_out,
+    hid_out,
+    gtok_out,
+    gr_out,
+    act_out,
+    dh_out,
+    n2_out,
+    c2_out,
+    stage,
+    send,
+    weights,
+    slots_in,
+    slots_out,
+    g1,
+    gc,
+    g2,
+    gm,
+    act1,
+    slope1,
+    dact2,
+    act2,
+    dh2,
+    dh1,
+    grads,
+    psend,
+    pown,
+    rcore,
+    s1,
+    rxy,
+    s2,
+    rz,
+    mid_ref,
+    gmid_ref,
+    stage_sem,
+    a2a_send,
+    a2a_recv,
+    slot_local,
+    slot_send,
+    slot_recv,
+    ag_send,
+    ag_recv,
+    rs_send,
+    rs_recv,
+    out_sem,
+):
+    rows, zs, xs, tok, width, units, per, slot_cap, tiles = dims
+    cols = zs * xs * 2
+    total = rows * cols
+    groups = rows * zs * xs
+    all_tok = total * tok
+    step = 256
+    unit_steps = units // step
+    width_steps = width // step
+    r = lax.axis_index("row")
+    c = lax.axis_index("col")
+    me = r * cols + c
+    core = lax.rem(c, 2)
+    x = lax.rem(c // 2, xs)
+    z = c // (2 * xs)
+    f32, bf16 = jnp.float32, jnp.bfloat16
+
+    def col_of(zi, xi, ci):
+        return (zi * xs + xi) * 2 + ci
+
+    def remote(src, dst, ssem, rsem, row_to, col_to):
+        return pltpu.make_async_remote_copy(
+            src_ref=src,
+            dst_ref=dst,
+            send_sem=ssem,
+            recv_sem=rsem,
+            device_id=(row_to, col_to),
+            device_id_type=MESH,
+        )
+
+    plane = [(dr, dx) for dr in range(rows) for dx in range(xs) if (dr, dx) != (0, 0)]
+
+    def ag_z(g, n):
+        out = []
+        for dz in range(1, zs):
+            zt = lax.rem(z + dz, zs)
+            here = g.at[r, z, x, core]
+            out.append(
+                remote(here, here, ag_send.at[n, dz], ag_recv.at[n, dz], r, col_of(zt, x, core))
+            )
+        for cp in out:
+            cp.start()
+        return out
+
+    def ag_xy(g, n):
+        out = []
+        for j, (dr, dx) in enumerate(plane):
+            rt, xt = lax.rem(r + dr, rows), lax.rem(x + dx, xs)
+            here = g.at[r, :, x, core]
+            out.append(
+                remote(
+                    here,
+                    here,
+                    ag_send.at[n, zs + j],
+                    ag_recv.at[n, zs + j],
+                    rt,
+                    col_of(z, xt, core),
+                )
+            )
+        for cp in out:
+            cp.start()
+        return out
+
+    def ag_core(g, n):
+        here = g.at[:, :, :, core]
+        cp = remote(here, here, ag_send.at[n, 0], ag_recv.at[n, 0], r, col_of(z, x, 1 - core))
+        cp.start()
+        return [cp]
+
+    def arrived(copies):
+        for cp in copies:
+            cp.wait_recv()
+
+    def flat_of(g, lo, size):
+        return g[:, :, :, :, :, lo : lo + size].reshape(all_tok, size)
+
+    def dot(a, b):
+        return jnp.dot(a, b, preferred_element_type=f32)
+
+    def rs_core(n, lhs, rhs):
+        def half(which, store):
+            left = lhs[:, pl.ds(which, 1)].reshape(groups * tok, units)
+
+            def tile(j, carry):
+                at = pl.ds(pl.multiple_of(j * step, step), step)
+                store(at, dot_nt(left, rhs(j)).reshape(groups, tok, step))
+                return carry
+
+            lax.fori_loop(0, width_steps, tile, 0)
+
+        def to_send(at, value):
+            psend[n, :, :, at] = value.astype(bf16)
+
+        def to_own(at, value):
+            pown[n, :, :, at] = value
+
+        half(1 - core, to_send)
+        cp = remote(
+            psend.at[n], rcore.at[n], rs_send.at[n, 0], rs_recv.at[n, 0], r, col_of(z, x, 1 - core)
+        )
+        cp.start()
+        half(core, to_own)
+        return [cp]
+
+    def rs_xy(n):
+        def add(k, carry):
+            value = pown[n, k] + rcore[n, k].astype(f32)
+            s1[n, k // (zs * xs), lax.rem(k // xs, zs), lax.rem(k, xs)] = value.astype(bf16)
+            return carry
+
+        lax.fori_loop(0, groups, add, 0)
+        out = []
+        for j, (dr, dx) in enumerate(plane):
+            rt, xt = lax.rem(r + dr, rows), lax.rem(x + dx, xs)
+            out.append(
+                remote(
+                    s1.at[n, rt, :, xt],
+                    rxy.at[n, j],
+                    rs_send.at[n, 1 + j],
+                    rs_recv.at[n, 1 + j],
+                    rt,
+                    col_of(z, xt, core),
+                )
+            )
+        for cp in out:
+            cp.start()
+        return out
+
+    def rs_z(n):
+        def add(k, carry):
+            value = s1[n, r, k, x].astype(f32)
+            for j in range(len(plane)):
+                value = value + rxy[n, j, k].astype(f32)
+            s2[n, k] = value.astype(bf16)
+            return carry
+
+        lax.fori_loop(0, zs, add, 0)
+        out = []
+        for dz in range(1, zs):
+            zt = lax.rem(z + dz, zs)
+            j = len(plane) + dz
+            out.append(
+                remote(
+                    s2.at[n, zt],
+                    rz.at[n, dz],
+                    rs_send.at[n, j],
+                    rs_recv.at[n, j],
+                    r,
+                    col_of(zt, x, core),
+                )
+            )
+        for cp in out:
+            cp.start()
+        return out
+
+    def rs_end(n):
+        value = s2[n, z].astype(f32)
+        for dz in range(1, zs):
+            value = value + rz[n, dz].astype(f32)
+        return value
+
+    def a2a_start(m, first):
+        def one(k, carry):
+            to = lax.rem(me + k, total)
+            rt, ct = to // cols, lax.rem(to, cols)
+            at = pl.ds(pl.multiple_of(me * per, per), per)
+            remote(send.at[m, rt, ct], weights.at[m, at], a2a_send.at[m], a2a_recv.at[m], rt, ct).start()
+            return carry
+
+        lax.fori_loop(first, total, one, 0)
+
+    def a2a_part(m):
+        span = weights.at[m, pl.ds(0, (total - 1) * per)]
+        return remote(span, span, a2a_send.at[m], a2a_recv.at[m], r, c)
+
+    def permute(m):
+        rows_in = cols * 16
+        p = lax.broadcasted_iota(jnp.int32, (rows_in, rows_in), 0)
+        q = lax.broadcasted_iota(jnp.int32, (rows_in, rows_in), 1)
+        swap = (lax.rem(p, 16) == q // cols) & (p // 16 == lax.rem(q, cols))
+        swap = jnp.where(swap, 1.0, 0.0).astype(bf16)
+
+        def block(k, carry):
+            b, h = k // unit_steps, lax.rem(k, unit_steps)
+            from_rows = pl.ds(pl.multiple_of(b * rows_in, rows_in), rows_in)
+            for rt in range(rows):
+                lanes = pl.ds(pl.multiple_of(rt * units + h * step, step), step)
+                got = dot(swap, stage[m, from_rows, lanes]).astype(bf16).reshape(cols, 16, step)
+                to_rows = pl.ds(pl.multiple_of(b * 16, 16), 16)
+                to_lanes = pl.ds(pl.multiple_of(h * step, step), step)
+                send[m, rt, :, to_rows, to_lanes] = got
+            return carry
+
+        lax.fori_loop(0, (per // 16) * unit_steps, block, 0)
+        weights[m, pl.ds(pl.multiple_of(me * per, per), per), :] = send[m, r, c]
+
+    loads = [
+        pltpu.make_async_copy(flat, stage.at[m], stage_sem.at[m])
+        for m, flat in enumerate((flat_in, flat_out))
+    ]
+    for cp in loads:
+        cp.start()
+
+    x_one = tok_ref[...].astype(f32)
+    inv_one = lax.rsqrt(jnp.mean(x_one * x_one, axis=1, keepdims=True) + norm_eps)
+    gain_one = gains_ref[0:1, :]
+    gain_two = gains_ref[1:2, :]
+    g1[r, z, x, core] = (x_one * inv_one * gain_one).astype(bf16)
+    gc[r, z, x, core] = gout_ref[...]
+    sent = []
+    one_z = ag_z(g1, 0)
+    cot_z = ag_z(gc, 1)
+
+    loads[0].wait()
+    permute(0)
+    arrived(one_z)
+    arrived(cot_z)
+    one_xy = ag_xy(g1, 0)
+    cot_xy = ag_xy(gc, 1)
+    a2a_start(0, 1)
+    loads[1].wait()
+    permute(1)
+    arrived(one_xy)
+    arrived(cot_xy)
+    one_c = ag_core(g1, 0)
+    cot_c = ag_core(gc, 1)
+    a2a_start(1, 1)
+
+    tile_refs = (tile_in, tile_out)
+    slots = (slots_in, slots_out)
+    slot_copies = []
+    for m in (1, 0):
+        for dr in range(rows):
+            rt = lax.rem(r + dr, rows)
+            src = tile_refs[m].at[0, :, :, pl.ds(pl.multiple_of(rt * units, units), units)]
+            if dr == 0:
+                cp = pltpu.make_async_copy(src, slots[m].at[r], slot_local.at[m])
+            else:
+                cp = remote(
+                    src, slots[m].at[r], slot_send.at[m, dr], slot_recv.at[m, dr], rt, c
+                )
+            cp.start()
+            slot_copies.append((m, dr, cp))
+
+    def slots_arrived(m):
+        for mm, dr, cp in slot_copies:
+            if mm == m:
+                if dr == 0:
+                    cp.wait()
+                else:
+                    cp.wait_recv()
+
+    arrived(one_c)
+    arrived(cot_c)
+    outs = []
+    for j, (src, dst) in enumerate(((gc, c2_out),)):
+        cp = pltpu.make_async_copy(src, dst, out_sem.at[0])
+        cp.start()
+        outs.append(cp)
+
+    a2a_part(0).wait_recv()
+
+    def hidden_one(j, carry):
+        at = pl.ds(pl.multiple_of(j * step, step), step)
+        act, slope = gelu_both(dot(flat_of(g1, 0, width), weights[0, :, at]))
+        act1[:, :, :, at] = act.astype(bf16).reshape(groups, 2, tok, step)
+        slope1[:, at] = slope
+        return carry
+
+    lax.fori_loop(0, unit_steps, hidden_one, 0)
+    a2a_part(1).wait_recv()
+
+    def out_rows(j):
+        return weights[1, pl.ds(pl.multiple_of(j * step, step), step), :]
+
+    def in_rows(j):
+        return weights[0, pl.ds(pl.multiple_of(j * step, step), step), :]
+
+    mix_c = rs_core(0, act1, out_rows)
+    arrived(mix_c)
+    mix_xy = rs_xy(0)
+
+    slots_arrived(1)
+
+    def cot_act(j, carry):
+        at = pl.ds(pl.multiple_of(j * step, step), step)
+        value = None
+        for k in range(tiles):
+            where = pick[tiles + k]
+            rhs = slots_out[where // slot_cap, lax.rem(where, slot_cap), :, at]
+            part = dot(flat_of(gc, k * step, step), rhs)
+            value = part if value is None else value + part
+        dact2[:, at] = value
+        return carry
+
+    arrived(mix_xy)
+    mix_z = rs_z(0)
+    lax.fori_loop(0, unit_steps, cot_act, 0)
+    arrived(mix_z)
+    middle = (x_one + rs_end(0)).astype(bf16)
+    mid_ref[...] = middle.astype(f32)
+    x_two = mid_ref[...]
+    inv_two = lax.rsqrt(jnp.mean(x_two * x_two, axis=1, keepdims=True) + norm_eps)
+    g2[r, z, x, core] = (x_two * inv_two * gain_two).astype(bf16)
+    two_z = ag_z(g2, 2)
+    arrived(two_z)
+    two_xy = ag_xy(g2, 2)
+    arrived(two_xy)
+    two_c = ag_core(g2, 2)
+    slots_arrived(0)
+    arrived(two_c)
+
+    def hidden_two(j, carry):
+        at = pl.ds(pl.multiple_of(j * step, step), step)
+        value = None
+        for k in range(tiles):
+            where = pick[k]
+            rhs = slots_in[where // slot_cap, lax.rem(where, slot_cap), :, at]
+            part = dot(flat_of(g2, k * step, step), rhs)
+            value = part if value is None else value + part
+        act, slope = gelu_both(value)
+        act2[:, :, :, at] = act.astype(bf16).reshape(groups, 2, tok, step)
+        dh2[:, :, :, at] = (dact2[:, at] * slope).astype(bf16).reshape(groups, 2, tok, step)
+        return carry
+
+    lax.fori_loop(0, unit_steps, hidden_two, 0)
+
+    def in_slot(k):
+        where = pick[k]
+        return slots_in[where // slot_cap, lax.rem(where, slot_cap)]
+
+    def out_slot(k):
+        where = pick[tiles + k]
+        return slots_out[where // slot_cap, lax.rem(where, slot_cap)]
+
+    back_c = rs_core(1, dh2, in_slot)
+    for j, (src, dst) in enumerate(((g2, n2_out), (act2, act_out), (dh2, dh_out))):
+        cp = pltpu.make_async_copy(src, dst, out_sem.at[1 + j])
+        cp.start()
+        outs.append(cp)
+    arrived(back_c)
+    back_xy = rs_xy(1)
+    last_c = rs_core(2, act2, out_slot)
+    arrived(back_xy)
+    back_z = rs_z(1)
+    arrived(last_c)
+    last_xy = rs_xy(2)
+    arrived(back_z)
+    gated = rs_end(1) * gain_two
+    mean = jnp.mean(x_two * gated, axis=1, keepdims=True)
+    grad_mid = (
+        gout_ref[...].astype(f32) + inv_two * gated - x_two * inv_two * inv_two * inv_two * mean
+    ).astype(bf16)
+    gm[r, z, x, core] = grad_mid
+    gmid_ref[...] = grad_mid.astype(f32)
+    cot_one_z = ag_z(gm, 3)
+    arrived(last_xy)
+    last_z = rs_z(2)
+    arrived(cot_one_z)
+    cot_one_xy = ag_xy(gm, 3)
+    arrived(last_z)
+    hid_out[...] = (x_two + rs_end(2)).astype(bf16)
+    arrived(cot_one_xy)
+    cot_one_c = ag_core(gm, 3)
+    arrived(cot_one_c)
+
+    def hidden_grad(j, carry):
+        at = pl.ds(pl.multiple_of(j * step, step), step)
+        value = dot(flat_of(gm, 0, width), weights[1, :, at]) * slope1[:, at]
+        dh1[:, :, :, at] = value.astype(bf16).reshape(groups, 2, tok, step)
+        return carry
+
+    lax.fori_loop(0, unit_steps, hidden_grad, 0)
+    first_c = rs_core(3, dh1, in_rows)
+
+    def weight_grad(m, left, right):
+        rhs = right[...].reshape(all_tok, units)
+
+        def tile(j, carry):
+            at = pl.ds(pl.multiple_of(j * step, step), step)
+            lhs = left[:, :, :, :, :, at].reshape(all_tok, step)
+            to = pl.ds(j * (step // per), step // per)
+            grads[m, to] = dot_tn(lhs, rhs).astype(bf16).reshape(step // per, per, units)
+            return carry
+
+        lax.fori_loop(0, width_steps, tile, 0)
+        cp = pltpu.make_async_copy(grads.at[m], gr_out.at[:, m], out_sem.at[4 + m])
+        cp.start()
+        outs.append(cp)
+
+    arrived(first_c)
+    first_xy = rs_xy(3)
+    weight_grad(1, gm, act1)
+    arrived(first_xy)
+    first_z = rs_z(3)
+    weight_grad(0, g1, dh1)
+    arrived(first_z)
+    gated = rs_end(3) * gain_one
+    mean = jnp.mean(x_one * gated, axis=1, keepdims=True)
+    gtok_out[...] = (
+        gmid_ref[...] + inv_one * gated - x_one * inv_one * inv_one * inv_one * mean
+    ).astype(bf16)
+
+    for cp in outs:
+        cp.wait()
+    for group in (
+        one_z, cot_z, one_xy, cot_xy, one_c, cot_c, mix_c, mix_xy, mix_z, two_z, two_xy, two_c,
+        back_c, back_xy, back_z, last_c, last_xy, last_z, cot_one_z, cot_one_xy, cot_one_c,
+        first_c, first_xy, first_z,
+    ):
+        for cp in group:
+            cp.wait_send()
+    for mm, dr, cp in slot_copies:
+        if dr > 0:
+            cp.wait_send()
+    a2a_part(0).wait_send()
+    a2a_part(1).wait_send()
+
+
+def middle_call(dims, pick, tokens, grad_out, gains, flat_in, flat_out, tile_in, tile_out):
+    rows, zs, xs, tok, width, units, per, slot_cap, tiles = dims
+    cols = zs * xs * 2
+    total = rows * cols
+    groups = rows * zs * xs
+    all_tok = total * tok
+    f32, bf16 = jnp.float32, jnp.bfloat16
+    shape = jax.ShapeDtypeStruct
+    vmem = pl.BlockSpec(memory_space=pltpu.VMEM)
+    hbm = pl.BlockSpec(memory_space=pl.ANY)
+    lane = (rows, zs, xs, 2, tok, width)
+    others = rows * xs
+    dma = pltpu.SemaphoreType.DMA
+    buf = pltpu.VMEM
+    return pl.pallas_call(
+        functools.partial(middle_kernel, dims),
+        in_specs=[pl.BlockSpec(memory_space=pltpu.SMEM), vmem, vmem, vmem, hbm, hbm, hbm, hbm],
+        out_specs=[vmem, vmem] + [hbm] * 5,
+        out_shape=[
+            shape((tok, width), bf16),
+            shape((tok, width), bf16),
+            shape((total, 2, per, units), bf16),
+            shape((groups, 2, tok, units), bf16),
+            shape((groups, 2, tok, units), bf16),
+            shape(lane, bf16),
+            shape(lane, bf16),
+        ],
+        scratch_shapes=[
+            buf((2,) + flat_in.shape, bf16),
+            buf((2, rows, cols, per, units), bf16),
+            buf((2, width, units), bf16),
+            buf((rows,) + tile_in.shape[1:3] + (units,), bf16),
+            buf((rows,) + tile_in.shape[1:3] + (units,), bf16),
+            buf(lane, bf16),
+            buf(lane, bf16),
+            buf(lane, bf16),
+            buf(lane, bf16),
+            buf((groups, 2, tok, units), bf16),
+            buf((all_tok, units), f32),
+            buf((all_tok, units), f32),
+            buf((groups, 2, tok, units), bf16),
+            buf((groups, 2, tok, units), bf16),
+            buf((groups, 2, tok, units), bf16),
+            buf((2, total, per, units), bf16),
+            buf((4, groups, tok, width), bf16),
+            buf((4, groups, tok, width), f32),
+            buf((4, groups, tok, width), bf16),
+            buf((4, rows, zs, xs, tok, width), bf16),
+            buf((4, others, zs, tok, width), bf16),
+            buf((4, zs, tok, width), bf16),
+            buf((4, zs, tok, width), bf16),
+            buf((tok, width), f32),
+            buf((tok, width), f32),
+            dma((2,)),
+            dma((2,)),
+            dma((2,)),
+            dma((2,)),
+            dma((2, rows)),
+            dma((2, rows)),
+            dma((4, zs + others)),
+            dma((4, zs + others)),
+            dma((4, zs + others)),
+            dma((4, zs + others)),
+            dma((6,)),
+        ],
+        compiler_params=pltpu.CompilerParams(
+            has_side_effects=True, vmem_limit_bytes=63 * 1024 * 1024
+        ),
+        cost_estimate=pl.CostEstimate(
+            flops=24 * all_tok * width * units, bytes_accessed=24 * width * units, transcendentals=0
+        ),
+        name="middle",
+    )(pick, tokens, grad_out, gains, flat_in, flat_out, tile_in, tile_out)
+
+
+def flat_both_kernel(cols, g, w_in, w_out, mom, sec, o_in, o_out, o_mom, o_sec):
+    rows_in, width = cols * 16, g.shape[-1]
+    p = lax.broadcasted_iota(jnp.int32, (rows_in, rows_in), 0)
+    q = lax.broadcasted_iota(jnp.int32, (rows_in, rows_in), 1)
+    swap = (lax.rem(p, cols) == q // 16) & (p // cols == lax.rem(q, 16))
+    swap = jnp.where(swap, 1.0, 0.0).astype(jnp.bfloat16)
+    for m, (w, o) in enumerate(((w_in, o_in), (w_out, o_out))):
+        got = g[0, :, m].reshape(rows_in, width)
+        grad = jnp.dot(swap, got, preferred_element_type=jnp.float32)
+        o[...], o_mom[m], o_sec[m] = adam_update(w[...], grad, mom[m], sec[m])
+
+
+def flat_both(w_in, w_out, g, mom, sec, dims):
+    rows, zs, xs, tok, width, units, per, slot_cap, tiles = dims
+    cols = zs * xs * 2
+    rows_in = cols * 16
+    step = min(units, 512)
+    parts = units // step
+    grid = (per // 16, rows * parts)
+    thin = pl.BlockSpec((rows_in, step), lambda i, j: (i, j))
+    wide = pl.BlockSpec((2, rows_in, step), lambda i, j: (0, i, j))
+    got = pl.BlockSpec((1, cols, 2, 16, step), lambda i, j: (j // parts, 0, 0, i, j % parts))
+    shape = jax.ShapeDtypeStruct
+    return pl.pallas_call(
+        functools.partial(flat_both_kernel, cols),
+        grid=grid,
+        in_specs=[got, thin, thin, wide, wide],
+        out_specs=[thin, thin, wide, wide],
+        out_shape=[
+            shape(w_in.shape, w_in.dtype),
+            shape(w_out.shape, w_out.dtype),
+            shape(mom.shape, mom.dtype),
+            shape(sec.shape, sec.dtype),
+        ],
+        cost_estimate=pl.CostEstimate(
+            flops=30 * mom.size, bytes_accessed=22 * mom.size, transcendentals=2 * mom.size
+        ),
+        name="flat_both",
+    )(g.reshape(rows, cols, 2, per, units), w_in, w_out, mom, sec)
+
+
+def slot_kernel(
+    tiles, live, l_in, l_out, r_in, r_out, w_in, w_out, mom, sec, o_in, o_out, o_mom, o_sec
+):
+    slot = pl.program_id(0)
+    step = w_in.shape[-1]
+    units = r_in.shape[-1]
+    at = pl.program_id(1) * step
+    row, lane = at // units, pl.multiple_of(lax.rem(at, units), step)
+    parts = ((l_in, r_in, w_in, o_in), (l_out, r_out, w_out, o_out))
+    for m, (left, right, w, o) in enumerate(parts):
+        grad = dot_tn(left[...], right[row, :, pl.ds(lane, step)])
+        alive = live[m, slot] > 0
+        old_w, old_m, old_s = w[0, 0], mom[m, 0, 0], sec[m, 0, 0]
+        new_w, new_m, new_s = adam_update(old_w, grad, old_m, old_s)
+        o[0, 0] = jnp.where(alive, new_w.astype(jnp.float32), old_w.astype(jnp.float32)).astype(
+            jnp.bfloat16
+        )
+        o_mom[m, 0, 0] = jnp.where(alive, new_m, old_m)
+        o_sec[m, 0, 0] = jnp.where(alive, new_s, old_s)
+
+
+def slot_adam(tiles, live, l_in, l_out, r_in, r_out, w_in, w_out, mom, sec):
+    slot_cap, tile_rows, width = w_in.shape[1:]
+    toks = l_in.shape[0]
+    step = min(r_in.shape[-1], 512)
+
+    def left_map(m):
+        return lambda s, h, tiles, live: (0, tiles[m, s])
+
+    def thin_map(s, h, *unused):
+        return (0, s, 0, h)
+
+    def wide_map(s, h, *unused):
+        return (0, 0, s, 0, h)
+
+    right = pl.BlockSpec(r_in.shape, lambda s, h, *unused: (0, 0, 0))
+    thin = pl.BlockSpec((1, 1, tile_rows, step), thin_map)
+    wide = pl.BlockSpec((2, 1, 1, tile_rows, step), wide_map)
+    shape = jax.ShapeDtypeStruct
+    return pl.pallas_call(
+        slot_kernel,
+        grid_spec=pltpu.PrefetchScalarGridSpec(
+            num_scalar_prefetch=2,
+            grid=(slot_cap, width // step),
+            in_specs=[
+                pl.BlockSpec((toks, tile_rows), left_map(0)),
+                pl.BlockSpec((toks, tile_rows), left_map(1)),
+                right,
+                right,
+                thin,
+                thin,
+                wide,
+                wide,
+            ],
+            out_specs=[thin, thin, wide, wide],
+        ),
+        out_shape=[
+            shape(w_in.shape, w_in.dtype),
+            shape(w_out.shape, w_out.dtype),
+            shape(mom.shape, mom.dtype),
+            shape(sec.shape, sec.dtype),
+        ],
+        cost_estimate=pl.CostEstimate(
+            flops=2 * toks * mom.size, bytes_accessed=22 * mom.size, transcendentals=mom.size
+        ),
+        name="slot_adam",
+    )(tiles, live, l_in, l_out, r_in, r_out, w_in, w_out, mom, sec)
+
+
+def fused_dims(row_total, col_total, tokens, flat_in, tile_in, owners):
+    depth = 4 if col_total % 8 == 0 else 1
+    across = col_total // (2 * depth)
+    total = row_total * col_total
+    tok, width = tokens.shape
+    units = flat_in.shape[1] // row_total
+    per = width // total
+    slot_cap, tile_rows = tile_in.shape[1:3]
+    tiles = owners.shape[-1]
+    fits = (
+        col_total % 2 == 0
+        and width % total == 0
+        and tok % 16 == 0
+        and per % 16 == 0
+        and units % 256 == 0
+        and tile_rows == 256
+        and tiles * tile_rows == width
+        and total * tok * (width * 30 + units * 16) + width * units * 24 < 60 * 2**20
+    )
+    return (row_total, depth, across, tok, width, units, per, slot_cap, tiles) if fits else None
+
+
+def fused_shards(
+    dims,
+    tokens,
+    grad_out,
+    gains,
+    flat_in,
+    flat_out,
+    flat_moment,
+    flat_second,
+    tile_in,
+    tile_out,
+    tile_moment,
+    tile_second,
+    owners,
+):
+    rows, zs, xs, tok, width, units, per, slot_cap, tiles = dims
+    cols = zs * xs * 2
+    all_tok = rows * cols * tok
+    row_index = lax.axis_index("row")
+    owner_rows = owners[:, 0, :]
+    ranks = tile_ranks(owner_rows)
+    pick = (owner_rows * slot_cap + ranks).reshape(-1).astype(jnp.int32)
+    slot_ids = jnp.arange(slot_cap, dtype=jnp.int32)[None, :, None]
+    mine = (owner_rows == row_index)[:, None, :] & (ranks[:, None, :] == slot_ids)
+    positions = jnp.arange(tiles, dtype=jnp.int32)
+    my_tiles = jnp.sum(jnp.where(mine, positions, 0), axis=-1).astype(jnp.int32)
+    my_live = jnp.any(mine, axis=-1).astype(jnp.int32)
+
+    hidden_out, grad_tokens, grads, act, d_hidden, normed, cot = middle_call(
+        dims, pick, tokens, grad_out, gains, flat_in, flat_out, tile_in, tile_out
+    )
+    act = act.reshape(all_tok, units)
+    d_hidden = d_hidden.reshape(all_tok, units)
+
+    def by_row(value):
+        got = [value]
+        for shift in range(1, rows):
+            pairs = [(src, (src + shift) % rows) for src in range(rows)]
+            got.append(lax.ppermute(value, "row", pairs))
+        ids = [lax.rem(row_index - shift + rows, rows) for shift in range(rows)]
+        if rows == 2:
+            first = row_index == 0
+            return jnp.stack([jnp.where(first, got[0], got[1]), jnp.where(first, got[1], got[0])])
+        placed = jnp.zeros((rows,) + value.shape, value.dtype)
+        for where, piece in zip(ids, got):
+            placed = lax.dynamic_update_index_in_dim(placed, piece, where, 0)
+        return placed
+
+    act_rows = by_row(act)
+    d_hidden_rows = by_row(d_hidden)
+
+    def spread(grad):
+        return lax.all_to_all(grad, both, split_axis=0, concat_axis=0, tiled=True)
+
+    pair = spread(grads.reshape(rows * cols, 2 * per, units))
+    new_tile = slot_adam(
+        my_tiles,
+        my_live,
+        normed.reshape(all_tok, width),
+        cot.reshape(all_tok, width),
+        d_hidden_rows,
+        act_rows,
+        tile_in,
+        tile_out,
+        tile_moment,
+        tile_second,
+    )
+    new_in, new_out, moment, second = flat_both(
+        flat_in, flat_out, pair, flat_moment, flat_second, dims
+    )
+    return (hidden_out, grad_tokens, new_in, new_out, moment, second, *new_tile)
 
 
 def solution(mesh):

time: 714 us -> 371 us (0.52)
  waiting for transfers between devices: 461 us -> 84.8 us
  Pallas kernels: 54.9 us -> 269 us
  blocking collectives: 61.1 us -> 0 us
  matrix products: 39 us -> 0 us
  local copies, waits for them, and re-layouts: 37.6 us -> 1.43 us
  starting transfers between devices: 22.1 us -> 5.82 us
  other arithmetic: 22.4 us -> 7.59 us
  between operations: 14.4 us -> 0.74 us
    pallas_call x2 -> x3, Pallas kernels: 54.9 us -> 269 us  [the longest x1 219 us: middle_call(): pl.pallas_call(functools.partial(middle_kernel, dims), in_specs=[pl.Block...]
    all_gather x4 -> x0, waiting for transfers between devices: 135 us -> none  [gather(): return lax.all_gather(x, both, axis=0, tiled=True)]
    reduce_scatter x2 -> x0, waiting for transfers between devices: 124 us -> none  [late_sum(): lax.psum_scatter(partial.astype(jnp.bfloat16), both, scatter_dimension=0,...]
    all_to_all x4 -> x1, waiting for transfers between devices: 80.4 us -> 0.01 us  [spread(): return lax.all_to_all(grad, both, split_axis=0, concat_axis=0, tiled=True)]
    all_to_all x2 -> x0, blocking collectives: 61.1 us -> none  [spread_sum(): came = lax.all_to_all(sent, both, split_axis=0, concat_axis=0, tiled=True)]
    dot_general x10 -> x0, matrix products: 39 us -> none  [the longest x4 12 us: dot_nt(): lax.dot_general(left, right, (((1,), (1,)), ((), ())), preferred_element_...]
    ppermute x4 -> x2, waiting for transfers between devices: 121 us -> 84.8 us  [by_row(): got.append(lax.ppermute(value, 'row', pairs))]
    all_to_all x4 -> x1, starting transfers between devices: 17.4 us -> 3.73 us  [spread(): return lax.all_to_all(grad, both, split_axis=0, concat_axis=0, tiled=True)]
  transfers between devices with their start and end apart: 14 -> 3, of which waited for: 10 -> 2; matrix products, arithmetic and copies ran while one was open for 10% -> 1% of each run, Pallas kernels for 4% -> 8%
where the time goes in v1:
time: 371 us; the launch traced here: 370 us
  Pallas kernels  269 us (73%)
  waiting for transfers between devices  84.8 us (23%)
  other arithmetic  7.59 us (2%)
  starting transfers between devices  5.82 us (2%)
    pallas_call x1, Pallas kernels, middle_call(): pl.pallas_call(functools.partial(middle_kernel, dims), in_specs=[pl.Block...  219 us
    ppermute x2, waiting for transfers between devices, by_row(): got.append(lax.ppermute(value, 'row', pairs))  84.8 us
    pallas_call x1, Pallas kernels, slot_adam(): pl.pallas_call(slot_kernel, grid_spec=pltpu.PrefetchScalarGridSpec(num_sc...  31.4 us
    pallas_call x1, Pallas kernels, flat_both(): pl.pallas_call(functools.partial(flat_both_kernel, cols), grid=grid, in_s...  19.2 us
  transfers between devices with their start and end apart: 3, of which 2 were waited for; matrix products, arithmetic and copies ran while one was open for 1% of the time, Pallas kernels for 8%

profile of v1, /device:TPU:0, one launch (start us, length us, event | category | flops | bytes accessed | tf_op | source)
XLA Modules:
  0.0 369.6 jit_solution(8842702580138739410)
XLA Ops:
  0.7 0.7 multiply_reduce_fusion
  1.4 1.0 select_reduce_fusion.1
  2.3 0.1 reduce_sum.21
  2.4 0.1 mul.8
  2.5 0.5 add.4.pick
  3.0 218.7 %middle.1 = (bf16[16,1024]{1,0:T(8,128)(2,1)}, bf16[16,1024]{1,0:T(8,128)(2,1)}, bf16[32,2,32,1024]{3,2,1,0:T(8,128)(2,1)}, bf16[16,2,16,1024]{3,2,1,0:T(8,128)(...) custom-call(s32[8]{0:T(128)} %add.4.pick, ...), custom_call_target="tpu_custom_call" | custom-call | flops 12884901888 | bytes 25165824 | tf_op jit(solution)/shard_map/middle/pallas_call | solution.py:813
  221.7 0.0 copy-start.1
  221.7 0.0 copy-start
  221.7 0.0 copy-start.4
  221.8 3.7 %all-to-all-start = ((bf16[32,64,1024]{2,1,0:T(8,128)(2,1)}), bf16[32,64,1024]{2,1,0:T(8,128)(2,1)}, u32[]{:S(2)}, u32[]{:S(2)}) async-start(bf16[32,64,1024]{2,1,0:T(8,128)(2,1)} %bitcast.22), calls=%async_computation | async-start | bytes 8388608 | tf_op jit(solution)/shard_map/all_to_all | solution.py:1058
  225.5 0.0 copy-done.1
  225.5 1.6 collective-permute-start.1
  227.2 0.0 copy-done
  227.2 0.4 collective-permute-start
  227.6 0.0 copy-done.4
  227.6 0.1 fusion.1
  227.8 0.6 convert_element_type.3.live
  228.3 0.7 select_reduce_fusion.tiles
  229.1 57.3 %collective-permute-done.1 = bf16[512,1024]{1,0:T(8,128)(2,1)} collective-permute-done((bf16[512,1024]{1,0:T(8,128)(2,1)S(1)}, bf16[512,1024]{1,0:T(8,128)(2,1)}, u32[]{:S(2)}, u32[]{:S(2)}) %collective-permute-start.1) | collective-permute-done | bytes 1048608 | tf_op jit(solution)/shard_map/ppermute | solution.py:1044
  286.3 1.4 select_bitcast_fusion.1
  287.7 27.5 %collective-permute-done = bf16[512,1024]{1,0:T(8,128)(2,1)S(1)} collective-permute-done((bf16[512,1024]{1,0:T(8,128)(2,1)S(1)}, bf16[512,1024]{1,0:T(8,128)(2,1)S(1)}, u32[]{:S(2)}, u32[]{:S(2)}) %collective-permute-start) | collective-permute-done | bytes 1048608 | tf_op jit(solution)/shard_map/ppermute | solution.py:1044
  315.2 0.2 select_bitcast_fusion.3
  315.4 2.4 pad_maximum_fusion
  317.8 31.4 %slot_adam.1 = (bf16[1,3,256,2048]{3,2,1,0:T(8,128)(2,1)}, bf16[1,3,256,2048]{3,2,1,0:T(8,128)(2,1)}, f32[2,1,3,256,2048]{4,3,2,1,0:T(8,128)}, f32[2,1,3,256,2048]{4,3,2,1,0:T(8,128)}) custom-call(s32[2,3]{1,0:T(2,128)} %select_reduce_fusion.tiles, s32[2,3]{1,0:T(2,128)} %convert_element_type.3.live, bf16[512,1024]{1,0:T(8,128)(2,1)} %bitcast.23, ...), custom_call_target="tpu_custom_call" | custom-call | flops 3221225472 | bytes 69206016 | tf_op jit(solution)/shard_map/slot_adam/pallas_call | solution.py:954
  349.1 0.0 all-to-all-done
  349.1 0.0 copy-start.3
  349.2 0.0 copy-start.2
  349.2 19.2 %flat_both.1 = (bf16[512,2048]{1,0:T(8,128)(2,1)}, bf16[512,2048]{1,0:T(8,128)(2,1)}, f32[2,512,2048]{2,1,0:T(8,128)}, f32[2,512,2048]{2,1,0:T(8,128)}) custom-call(bf16[2,16,2,32,1024]{4,3,2,1,0:T(8,128)(2,1)} %bitcast.2.g, bf16[512,2048]{1,0:T(8,128)(2,1)} %w_in.2, bf16[512,2048]{1,0:T(8,128)(2,1)} %w_out.2, f32[2,512,2048]{2,1,0:T(8,128)} %mom.2, ...), custom_call_target="tpu_custom_call" | custom-call | flops 62914560 | bytes 46137344 | tf_op jit(solution)/shard_map/flat_both/pallas_call | solution.py:897
  368.3 0.0 copy-done.3
  368.4 0.6 copy.30
  369.0 0.0 copy-done.2
  369.0 0.6 copy.31
  (3 shorter events, 0.0 us)
Async XLA Ops:
  221.7 3.8 %copy-start.1 = (bf16[16,2,16,1024]{3,2,1,0:T(8,128)(2,1)S(1)}, bf16[16,2,16,1024]{3,2,1,0:T(8,128)(2,1)}, u32[]{:S(2)}) copy-start(bf16[16,2,16,1024]{3,2,1,0:T(8,128)(2,1)} %get-tuple-element.35) | copy-start | bytes 3145732
  221.7 5.4 %copy-start = (bf16[16,2,16,1024]{3,2,1,0:T(8,128)(2,1)S(1)}, bf16[16,2,16,1024]{3,2,1,0:T(8,128)(2,1)}, u32[]{:S(2)}) copy-start(bf16[16,2,16,1024]{3,2,1,0:T(8,128)(2,1)} %get-tuple-element.34) | copy-start | bytes 3145732
  221.7 5.9 %copy-start.4 = (s32[2,1,4]{2,1,0:T(1,128)S(1)}, s32[2,1,4]{2,1,0:T(1,128)}, u32[]{:S(2)}) copy-start(s32[2,1,4]{2,1,0:T(1,128)} %param.23) | copy-start | bytes 100
  221.8 127.4 %all-to-all-start = ((bf16[32,64,1024]{2,1,0:T(8,128)(2,1)}), bf16[32,64,1024]{2,1,0:T(8,128)(2,1)}, u32[]{:S(2)}, u32[]{:S(2)}) async-start(bf16[32,64,1024]{2,1,0:T(8,128)(2,1)} %bitcast.22), calls=%async_computation | async-start | bytes 8388608 | tf_op jit(solution)/shard_map/all_to_all | solution.py:1058
  225.5 60.8 %collective-permute-start.1 = (bf16[512,1024]{1,0:T(8,128)(2,1)S(1)}, bf16[512,1024]{1,0:T(8,128)(2,1)}, u32[]{:S(2)}, u32[]{:S(2)}) collective-permute-start(bf16[512,1024]{1,0:T(8,128)(2,1)S(1)} %bitcast.26), channel_id=1, source_target_pairs={{0,16},{16,0},{1,17},{17,1},{2,18},{18,2},{3,19},{19,3},{4,20},{20... | collective-permute-start | bytes 3145736 | tf_op jit(solution)/shard_map/ppermute | solution.py:1044
  227.2 88.0 %collective-permute-start = (bf16[512,1024]{1,0:T(8,128)(2,1)S(1)}, bf16[512,1024]{1,0:T(8,128)(2,1)S(1)}, u32[]{:S(2)}, u32[]{:S(2)}) collective-permute-start(bf16[512,1024]{1,0:T(8,128)(2,1)S(1)} %bitcast.25), channel_id=1, source_target_pairs={{0,16},{16,0},{1,17},{17,1},{2,18},{18,2},{3,19},{19,3},{4,20},{20... | collective-permute-start | bytes 3145736 | tf_op jit(solution)/shard_map/ppermute | solution.py:1044
  349.1 19.2 %copy-start.3 = (bf16[16,1024]{1,0:T(8,128)(2,1)S(1)}, bf16[16,1024]{1,0:T(8,128)(2,1)}, u32[]{:S(2)}) copy-start(bf16[16,1024]{1,0:T(8,128)(2,1)} %get-tuple-element.56) | copy-start | bytes 98308
  349.2 19.8 %copy-start.2 = (bf16[16,1024]{1,0:T(8,128)(2,1)S(1)}, bf16[16,1024]{1,0:T(8,128)(2,1)}, u32[]{:S(2)}) copy-start(bf16[16,1024]{1,0:T(8,128)(2,1)} %get-tuple-element.57) | copy-start | bytes 98308

commit v2 on v1

--- a/solution.py
+++ b/solution.py
@@ -32,7 +32,7 @@
     new_second = beta_two * second + (1.0 - beta_two) * gradient * gradient
     weight_float = weight.astype(jnp.float32)
     stepped = weight_float - learn_rate * (
-        new_moment / (jnp.sqrt(new_second) + adam_eps) + decay_rate * weight_float
+        new_moment / (new_second * lax.rsqrt(new_second) + adam_eps) + decay_rate * weight_float
     )
     return (stepped.astype(jnp.bfloat16), new_moment, new_second)
 
@@ -345,7 +345,9 @@
     send,
     weights,
     slots_in,
-    slots_out,
+    own_out,
+    cot_send,
+    cot_far,
     g1,
     gc,
     g2,
@@ -354,6 +356,7 @@
     slope1,
     dact2,
     act2,
+    act2_far,
     dh2,
     dh1,
     grads,
@@ -376,6 +379,10 @@
     ag_recv,
     rs_send,
     rs_recv,
+    act_send,
+    act_recv,
+    cot_ssem,
+    cot_rsem,
     out_sem,
 ):
     rows, zs, xs, tok, width, units, per, slot_cap, tiles = dims
@@ -407,6 +414,7 @@
             device_id_type=MESH,
         )
 
+    sent = []
     plane = [(dr, dx) for dr in range(rows) for dx in range(xs) if (dr, dx) != (0, 0)]
 
     def ag_z(g, n):
@@ -419,6 +427,7 @@
             )
         for cp in out:
             cp.start()
+        sent.extend(out)
         return out
 
     def ag_xy(g, n):
@@ -438,12 +447,14 @@
             )
         for cp in out:
             cp.start()
+        sent.extend(out)
         return out
 
     def ag_core(g, n):
         here = g.at[:, :, :, core]
         cp = remote(here, here, ag_send.at[n, 0], ag_recv.at[n, 0], r, col_of(z, x, 1 - core))
         cp.start()
+        sent.append(cp)
         return [cp]
 
     def arrived(copies):
@@ -456,13 +467,19 @@
     def dot(a, b):
         return jnp.dot(a, b, preferred_element_type=f32)
 
-    def rs_core(n, lhs, rhs):
+    def rs_core(n, lhs, rhs, own=None):
         def half(which, store):
-            left = lhs[:, pl.ds(which, 1)].reshape(groups * tok, units)
+            left = [lh[:, pl.ds(which, 1)].reshape(groups * tok, units) for lh in lhs]
 
             def tile(j, carry):
                 at = pl.ds(pl.multiple_of(j * step, step), step)
-                store(at, dot_nt(left, rhs(j)).reshape(groups, tok, step))
+                value = None
+                for lh, rh in zip(left, rhs):
+                    part = dot_nt(lh, rh(j))
+                    value = part if value is None else value + part
+                if own is not None:
+                    value = jnp.where(own(j), value, 0.0)
+                store(at, value.reshape(groups, tok, step))
                 return carry
 
             lax.fori_loop(0, width_steps, tile, 0)
@@ -478,6 +495,7 @@
             psend.at[n], rcore.at[n], rs_send.at[n, 0], rs_recv.at[n, 0], r, col_of(z, x, 1 - core)
         )
         cp.start()
+        sent.append(cp)
         half(core, to_own)
         return [cp]
 
@@ -503,6 +521,7 @@
             )
         for cp in out:
             cp.start()
+        sent.extend(out)
         return out
 
     def rs_z(n):
@@ -530,6 +549,7 @@
             )
         for cp in out:
             cp.start()
+        sent.extend(out)
         return out
 
     def rs_end(n):
@@ -559,18 +579,20 @@
         swap = (lax.rem(p, 16) == q // cols) & (p // 16 == lax.rem(q, cols))
         swap = jnp.where(swap, 1.0, 0.0).astype(bf16)
 
+        wide = min(units, 512)
+
         def block(k, carry):
-            b, h = k // unit_steps, lax.rem(k, unit_steps)
+            b, h = k // (units // wide), lax.rem(k, units // wide)
             from_rows = pl.ds(pl.multiple_of(b * rows_in, rows_in), rows_in)
+            to_rows = pl.ds(pl.multiple_of(b * 16, 16), 16)
+            to_lanes = pl.ds(pl.multiple_of(h * wide, wide), wide)
             for rt in range(rows):
-                lanes = pl.ds(pl.multiple_of(rt * units + h * step, step), step)
-                got = dot(swap, stage[m, from_rows, lanes]).astype(bf16).reshape(cols, 16, step)
-                to_rows = pl.ds(pl.multiple_of(b * 16, 16), 16)
-                to_lanes = pl.ds(pl.multiple_of(h * step, step), step)
+                lanes = pl.ds(pl.multiple_of(rt * units + h * wide, wide), wide)
+                got = dot(swap, stage[m, from_rows, lanes]).astype(bf16).reshape(cols, 16, wide)
                 send[m, rt, :, to_rows, to_lanes] = got
             return carry
 
-        lax.fori_loop(0, (per // 16) * unit_steps, block, 0)
+        lax.fori_loop(0, (per // 16) * (units // wide), block, 0)
         weights[m, pl.ds(pl.multiple_of(me * per, per), per), :] = send[m, r, c]
 
     loads = [
@@ -580,54 +602,59 @@
     for cp in loads:
         cp.start()
 
+    slot_copies = []
+    half_rows = slots_in.shape[2] // 2
+    my_lanes = pl.ds(pl.multiple_of(r * units, units), units)
+    slot_loads = [
+        pltpu.make_async_copy(tile_in.at[0, :, :, my_lanes], slots_in.at[r], slot_local.at[0]),
+        pltpu.make_async_copy(tile_out.at[0], own_out, slot_local.at[1]),
+    ]
+    for cp in slot_loads:
+        cp.start()
+
+    def lanes_of(dr):
+        return pl.ds(pl.multiple_of(lax.rem(r + dr, rows) * units, units), units)
+
+    def slots_start(first, last):
+        for q in range(first, last):
+            slot, part = q // 2, pl.ds(q % 2 * half_rows, half_rows)
+            for dr in range(1, rows):
+                cp = remote(
+                    tile_in.at[0, slot, part, lanes_of(dr)],
+                    slots_in.at[r, slot, part],
+                    slot_send.at[dr, q],
+                    slot_recv.at[dr, q],
+                    lax.rem(r + dr, rows),
+                    c,
+                )
+                sent.append(cp)
+                cp.start()
+                slot_copies.append(cp)
+
     x_one = tok_ref[...].astype(f32)
     inv_one = lax.rsqrt(jnp.mean(x_one * x_one, axis=1, keepdims=True) + norm_eps)
     gain_one = gains_ref[0:1, :]
     gain_two = gains_ref[1:2, :]
     g1[r, z, x, core] = (x_one * inv_one * gain_one).astype(bf16)
     gc[r, z, x, core] = gout_ref[...]
-    sent = []
     one_z = ag_z(g1, 0)
     cot_z = ag_z(gc, 1)
-
+    slots_start(0, 1)
     loads[0].wait()
     permute(0)
     arrived(one_z)
+    one_xy = ag_xy(g1, 0)
     arrived(cot_z)
-    one_xy = ag_xy(g1, 0)
     cot_xy = ag_xy(gc, 1)
     a2a_start(0, 1)
+    slots_start(1, 2 * slot_cap)
     loads[1].wait()
     permute(1)
+    a2a_start(1, 1)
     arrived(one_xy)
+    one_c = ag_core(g1, 0)
     arrived(cot_xy)
-    one_c = ag_core(g1, 0)
     cot_c = ag_core(gc, 1)
-    a2a_start(1, 1)
-
-    tile_refs = (tile_in, tile_out)
-    slots = (slots_in, slots_out)
-    slot_copies = []
-    for m in (1, 0):
-        for dr in range(rows):
-            rt = lax.rem(r + dr, rows)
-            src = tile_refs[m].at[0, :, :, pl.ds(pl.multiple_of(rt * units, units), units)]
-            if dr == 0:
-                cp = pltpu.make_async_copy(src, slots[m].at[r], slot_local.at[m])
-            else:
-                cp = remote(
-                    src, slots[m].at[r], slot_send.at[m, dr], slot_recv.at[m, dr], rt, c
-                )
-            cp.start()
-            slot_copies.append((m, dr, cp))
-
-    def slots_arrived(m):
-        for mm, dr, cp in slot_copies:
-            if mm == m:
-                if dr == 0:
-                    cp.wait()
-                else:
-                    cp.wait_recv()
 
     arrived(one_c)
     arrived(cot_c)
@@ -637,6 +664,49 @@
         cp.start()
         outs.append(cp)
 
+    slot_loads[1].wait()
+
+    def cot_tile(store, lanes0, j):
+        value = None
+        for k in range(tiles):
+            flag = jnp.where(pick[2 * tiles + k] > 0, 1.0, 0.0).astype(bf16)
+            lanes = pl.ds(pl.multiple_of(lanes0 + j * step, step), step)
+            part = dot(flat_of(gc, k * step, step), own_out[pick[tiles + k], :, lanes] * flag)
+            value = part if value is None else value + part
+        store(pl.ds(pl.multiple_of(j * step, step), step), value)
+
+    cot_copies = []
+    for dr in range(1, rows):
+
+        def cot_other(j, carry, dr=dr):
+            def store(at, value):
+                cot_send[dr - 1, :, at] = value.astype(bf16)
+
+            cot_tile(store, lax.rem(r + dr, rows) * units, j)
+            return carry
+
+        lax.fori_loop(0, unit_steps, cot_other, 0)
+        cp = remote(
+            cot_send.at[dr - 1],
+            cot_far.at[dr - 1],
+            cot_ssem.at[dr],
+            cot_rsem.at[dr],
+            lax.rem(r + dr, rows),
+            c,
+        )
+        cp.start()
+        sent.append(cp)
+        cot_copies.append(cp)
+
+    def cot_mine(j, carry):
+        def store(at, value):
+            dact2[:, at] = value
+
+        cot_tile(store, r * units, j)
+        return carry
+
+    lax.fori_loop(0, unit_steps, cot_mine, 0)
+
     a2a_part(0).wait_recv()
 
     def hidden_one(j, carry):
@@ -655,38 +725,27 @@
     def in_rows(j):
         return weights[0, pl.ds(pl.multiple_of(j * step, step), step), :]
 
-    mix_c = rs_core(0, act1, out_rows)
+    mix_c = rs_core(0, [act1], [out_rows])
     arrived(mix_c)
     mix_xy = rs_xy(0)
 
-    slots_arrived(1)
-
-    def cot_act(j, carry):
-        at = pl.ds(pl.multiple_of(j * step, step), step)
-        value = None
-        for k in range(tiles):
-            where = pick[tiles + k]
-            rhs = slots_out[where // slot_cap, lax.rem(where, slot_cap), :, at]
-            part = dot(flat_of(gc, k * step, step), rhs)
-            value = part if value is None else value + part
-        dact2[:, at] = value
-        return carry
-
     arrived(mix_xy)
     mix_z = rs_z(0)
-    lax.fori_loop(0, unit_steps, cot_act, 0)
     arrived(mix_z)
     middle = (x_one + rs_end(0)).astype(bf16)
     mid_ref[...] = middle.astype(f32)
     x_two = mid_ref[...]
     inv_two = lax.rsqrt(jnp.mean(x_two * x_two, axis=1, keepdims=True) + norm_eps)
     g2[r, z, x, core] = (x_two * inv_two * gain_two).astype(bf16)
+
     two_z = ag_z(g2, 2)
     arrived(two_z)
     two_xy = ag_xy(g2, 2)
     arrived(two_xy)
     two_c = ag_core(g2, 2)
-    slots_arrived(0)
+    slot_loads[0].wait()
+    arrived(slot_copies)
+    arrived(cot_copies)
     arrived(two_c)
 
     def hidden_two(j, carry):
@@ -699,7 +758,10 @@
             value = part if value is None else value + part
         act, slope = gelu_both(value)
         act2[:, :, :, at] = act.astype(bf16).reshape(groups, 2, tok, step)
-        dh2[:, :, :, at] = (dact2[:, at] * slope).astype(bf16).reshape(groups, 2, tok, step)
+        d_act = dact2[:, at]
+        for dr in range(1, rows):
+            d_act = d_act + cot_far[dr - 1, :, at].astype(f32)
+        dh2[:, :, :, at] = (d_act * slope).astype(bf16).reshape(groups, 2, tok, step)
         return carry
 
     lax.fori_loop(0, unit_steps, hidden_two, 0)
@@ -708,22 +770,37 @@
         where = pick[k]
         return slots_in[where // slot_cap, lax.rem(where, slot_cap)]
 
-    def out_slot(k):
-        where = pick[tiles + k]
-        return slots_out[where // slot_cap, lax.rem(where, slot_cap)]
-
-    back_c = rs_core(1, dh2, in_slot)
-    for j, (src, dst) in enumerate(((g2, n2_out), (act2, act_out), (dh2, dh_out))):
+    act_copies = []
+    piece = groups // 4
+
+    def act_start(q):
+        for dr in range(1, rows):
+            span = pl.ds(q * piece, piece)
+            cp = remote(
+                act2.at[span],
+                act2_far.at[dr - 1, span],
+                act_send.at[dr, q],
+                act_recv.at[dr, q],
+                lax.rem(r + dr, rows),
+                c,
+            )
+            cp.start()
+            sent.append(cp)
+            act_copies.append(cp)
+
+    act_start(0)
+    act_start(1)
+    back_c = rs_core(1, [dh2], [in_slot])
+    for j, (src, dst) in enumerate(((g2, n2_out), (act2, act_out.at[r]), (dh2, dh_out))):
         cp = pltpu.make_async_copy(src, dst, out_sem.at[1 + j])
         cp.start()
         outs.append(cp)
     arrived(back_c)
     back_xy = rs_xy(1)
-    last_c = rs_core(2, act2, out_slot)
     arrived(back_xy)
     back_z = rs_z(1)
-    arrived(last_c)
-    last_xy = rs_xy(2)
+    act_start(2)
+    act_start(3)
     arrived(back_z)
     gated = rs_end(1) * gain_two
     mean = jnp.mean(x_two * gated, axis=1, keepdims=True)
@@ -733,14 +810,32 @@
     gm[r, z, x, core] = grad_mid
     gmid_ref[...] = grad_mid.astype(f32)
     cot_one_z = ag_z(gm, 3)
-    arrived(last_xy)
-    last_z = rs_z(2)
     arrived(cot_one_z)
     cot_one_xy = ag_xy(gm, 3)
-    arrived(last_z)
-    hid_out[...] = (x_two + rs_end(2)).astype(bf16)
+
+    def out_slot(dr):
+        return lambda k: own_out[pick[tiles + k], :, lanes_of(dr)]
+
+    def mine(k):
+        return pick[2 * tiles + k] > 0
+
+    arrived(act_copies)
+    last_c = rs_core(
+        2,
+        [act2] + [act2_far.at[dr - 1] for dr in range(1, rows)],
+        [out_slot((rows - dr) % rows) for dr in range(rows)],
+        mine,
+    )
     arrived(cot_one_xy)
     cot_one_c = ag_core(gm, 3)
+    for dr in range(1, rows):
+        cp = pltpu.make_async_copy(
+            act2_far.at[dr - 1], act_out.at[lax.rem(r + rows - dr, rows)], out_sem.at[5 + dr]
+        )
+        cp.start()
+        outs.append(cp)
+    arrived(last_c)
+    last_xy = rs_xy(2)
     arrived(cot_one_c)
 
     def hidden_grad(j, carry):
@@ -750,7 +845,7 @@
         return carry
 
     lax.fori_loop(0, unit_steps, hidden_grad, 0)
-    first_c = rs_core(3, dh1, in_rows)
+    first_c = rs_core(3, [dh1], [in_rows])
 
     def weight_grad(m, left, right):
         rhs = right[...].reshape(all_tok, units)
@@ -767,9 +862,13 @@
         cp.start()
         outs.append(cp)
 
+    arrived(last_xy)
+    last_z = rs_z(2)
     arrived(first_c)
     first_xy = rs_xy(3)
     weight_grad(1, gm, act1)
+    arrived(last_z)
+    hid_out[...] = (x_two + rs_end(2)).astype(bf16)
     arrived(first_xy)
     first_z = rs_z(3)
     weight_grad(0, g1, dh1)
@@ -782,16 +881,8 @@
 
     for cp in outs:
         cp.wait()
-    for group in (
-        one_z, cot_z, one_xy, cot_xy, one_c, cot_c, mix_c, mix_xy, mix_z, two_z, two_xy, two_c,
-        back_c, back_xy, back_z, last_c, last_xy, last_z, cot_one_z, cot_one_xy, cot_one_c,
-        first_c, first_xy, first_z,
-    ):
-        for cp in group:
-            cp.wait_send()
-    for mm, dr, cp in slot_copies:
-        if dr > 0:
-            cp.wait_send()
+    for cp in sent:
+        cp.wait_send()
     a2a_part(0).wait_send()
     a2a_part(1).wait_send()
 
@@ -818,7 +909,7 @@
             shape((tok, width), bf16),
             shape((tok, width), bf16),
             shape((total, 2, per, units), bf16),
-            shape((groups, 2, tok, units), bf16),
+            shape((rows, groups, 2, tok, units), bf16),
             shape((groups, 2, tok, units), bf16),
             shape(lane, bf16),
             shape(lane, bf16),
@@ -828,7 +919,9 @@
             buf((2, rows, cols, per, units), bf16),
             buf((2, width, units), bf16),
             buf((rows,) + tile_in.shape[1:3] + (units,), bf16),
-            buf((rows,) + tile_in.shape[1:3] + (units,), bf16),
+            buf(tile_out.shape[1:], bf16),
+            buf((rows - 1, all_tok, units), bf16),
+            buf((rows - 1, all_tok, units), bf16),
             buf(lane, bf16),
             buf(lane, bf16),
             buf(lane, bf16),
@@ -837,6 +930,7 @@
             buf((all_tok, units), f32),
             buf((all_tok, units), f32),
             buf((groups, 2, tok, units), bf16),
+            buf((rows - 1, groups, 2, tok, units), bf16),
             buf((groups, 2, tok, units), bf16),
             buf((groups, 2, tok, units), bf16),
             buf((2, total, per, units), bf16),
@@ -853,13 +947,17 @@
             dma((2,)),
             dma((2,)),
             dma((2,)),
-            dma((2, rows)),
-            dma((2, rows)),
+            dma((rows, 2 * slot_cap)),
+            dma((rows, 2 * slot_cap)),
             dma((4, zs + others)),
             dma((4, zs + others)),
             dma((4, zs + others)),
             dma((4, zs + others)),
-            dma((6,)),
+            dma((rows, 4)),
+            dma((rows, 4)),
+            dma((rows,)),
+            dma((rows,)),
+            dma((6 + rows,)),
         ],
         compiler_params=pltpu.CompilerParams(
             has_side_effects=True, vmem_limit_bytes=63 * 1024 * 1024
@@ -871,32 +969,36 @@
     )(pick, tokens, grad_out, gains, flat_in, flat_out, tile_in, tile_out)
 
 
-def flat_both_kernel(cols, g, w_in, w_out, mom, sec, o_in, o_out, o_mom, o_sec):
-    rows_in, width = cols * 16, g.shape[-1]
-    p = lax.broadcasted_iota(jnp.int32, (rows_in, rows_in), 0)
-    q = lax.broadcasted_iota(jnp.int32, (rows_in, rows_in), 1)
+def flat_both_kernel(cols, split, g, w_in, w_out, mom, sec, o_in, o_out, o_mom, o_sec):
+    rows, units = g.shape[0], g.shape[-1]
+    rows_in = cols * 16
+    part = rows_in // split
+    p = lax.broadcasted_iota(jnp.int32, (part, rows_in), 0) + pl.program_id(1) * part
+    q = lax.broadcasted_iota(jnp.int32, (part, rows_in), 1)
     swap = (lax.rem(p, cols) == q // 16) & (p // cols == lax.rem(q, 16))
     swap = jnp.where(swap, 1.0, 0.0).astype(jnp.bfloat16)
     for m, (w, o) in enumerate(((w_in, o_in), (w_out, o_out))):
-        got = g[0, :, m].reshape(rows_in, width)
-        grad = jnp.dot(swap, got, preferred_element_type=jnp.float32)
-        o[...], o_mom[m], o_sec[m] = adam_update(w[...], grad, mom[m], sec[m])
+        for rt in range(rows):
+            at = slice(rt * units, (rt + 1) * units)
+            got = g[rt, :, m].reshape(rows_in, units)
+            grad = jnp.dot(swap, got, preferred_element_type=jnp.float32)
+            new = adam_update(w[:, at], grad, mom[m, :, at], sec[m, :, at])
+            o[:, at], o_mom[m, :, at], o_sec[m, :, at] = new
 
 
 def flat_both(w_in, w_out, g, mom, sec, dims):
     rows, zs, xs, tok, width, units, per, slot_cap, tiles = dims
     cols = zs * xs * 2
-    rows_in = cols * 16
-    step = min(units, 512)
-    parts = units // step
-    grid = (per // 16, rows * parts)
-    thin = pl.BlockSpec((rows_in, step), lambda i, j: (i, j))
-    wide = pl.BlockSpec((2, rows_in, step), lambda i, j: (0, i, j))
-    got = pl.BlockSpec((1, cols, 2, 16, step), lambda i, j: (j // parts, 0, 0, i, j % parts))
+    split = 2
+    part = cols * 16 // split
+    block = rows * units
+    thin = pl.BlockSpec((part, block), lambda i, h: (i * split + h, 0))
+    wide = pl.BlockSpec((2, part, block), lambda i, h: (0, i * split + h, 0))
+    got = pl.BlockSpec((rows, cols, 2, 16, units), lambda i, h: (0, 0, 0, i, 0))
     shape = jax.ShapeDtypeStruct
     return pl.pallas_call(
-        functools.partial(flat_both_kernel, cols),
-        grid=grid,
+        functools.partial(flat_both_kernel, cols, split),
+        grid=(per // 16, split),
         in_specs=[got, thin, thin, wide, wide],
         out_specs=[thin, thin, wide, wide],
         out_shape=[
@@ -912,73 +1014,57 @@
     )(g.reshape(rows, cols, 2, per, units), w_in, w_out, mom, sec)
 
 
-def slot_kernel(
-    tiles, live, l_in, l_out, r_in, r_out, w_in, w_out, mom, sec, o_in, o_out, o_mom, o_sec
-):
+def slot_kernel_part(m, tiles, live, left, right, w, mom, sec, *rest):
+    o, o_mom, o_sec = rest[-3:]
     slot = pl.program_id(0)
-    step = w_in.shape[-1]
-    units = r_in.shape[-1]
+    step = w.shape[-1]
+    units = right.shape[-1]
     at = pl.program_id(1) * step
     row, lane = at // units, pl.multiple_of(lax.rem(at, units), step)
-    parts = ((l_in, r_in, w_in, o_in), (l_out, r_out, w_out, o_out))
-    for m, (left, right, w, o) in enumerate(parts):
-        grad = dot_tn(left[...], right[row, :, pl.ds(lane, step)])
-        alive = live[m, slot] > 0
-        old_w, old_m, old_s = w[0, 0], mom[m, 0, 0], sec[m, 0, 0]
-        new_w, new_m, new_s = adam_update(old_w, grad, old_m, old_s)
-        o[0, 0] = jnp.where(alive, new_w.astype(jnp.float32), old_w.astype(jnp.float32)).astype(
-            jnp.bfloat16
-        )
-        o_mom[m, 0, 0] = jnp.where(alive, new_m, old_m)
-        o_sec[m, 0, 0] = jnp.where(alive, new_s, old_s)
-
-
-def slot_adam(tiles, live, l_in, l_out, r_in, r_out, w_in, w_out, mom, sec):
-    slot_cap, tile_rows, width = w_in.shape[1:]
-    toks = l_in.shape[0]
-    step = min(r_in.shape[-1], 512)
-
-    def left_map(m):
-        return lambda s, h, tiles, live: (0, tiles[m, s])
-
-    def thin_map(s, h, *unused):
-        return (0, s, 0, h)
-
-    def wide_map(s, h, *unused):
-        return (0, 0, s, 0, h)
-
-    right = pl.BlockSpec(r_in.shape, lambda s, h, *unused: (0, 0, 0))
-    thin = pl.BlockSpec((1, 1, tile_rows, step), thin_map)
-    wide = pl.BlockSpec((2, 1, 1, tile_rows, step), wide_map)
+    grad = dot_tn(left[...], right[row, :, pl.ds(lane, step)])
+    alive = live[m, slot] > 0
+    old_w, old_m, old_s = w[0, 0], mom[0, 0, 0], sec[0, 0, 0]
+    new_w, new_m, new_s = adam_update(old_w, grad, old_m, old_s)
+    o[0, 0] = jnp.where(alive, new_w.astype(jnp.float32), old_w.astype(jnp.float32)).astype(
+        jnp.bfloat16
+    )
+    o_mom[0, 0, 0] = jnp.where(alive, new_m, old_m)
+    o_sec[0, 0, 0] = jnp.where(alive, new_s, old_s)
+
+
+def slot_part(m, tiles, live, left, right, w, mom, sec, before=()):
+    slot_cap, tile_rows, width = w.shape[1:]
+    toks = left.shape[0]
+    step = min(right.shape[-1], 1024)
+    thin = pl.BlockSpec((1, 1, tile_rows, step), lambda s, h, *unused: (0, s, 0, h))
+    wide = pl.BlockSpec((1, 1, 1, tile_rows, step), lambda s, h, *unused: (m, 0, s, 0, h))
     shape = jax.ShapeDtypeStruct
     return pl.pallas_call(
-        slot_kernel,
+        functools.partial(slot_kernel_part, m),
         grid_spec=pltpu.PrefetchScalarGridSpec(
             num_scalar_prefetch=2,
             grid=(slot_cap, width // step),
             in_specs=[
-                pl.BlockSpec((toks, tile_rows), left_map(0)),
-                pl.BlockSpec((toks, tile_rows), left_map(1)),
-                right,
-                right,
-                thin,
+                pl.BlockSpec((toks, tile_rows), lambda s, h, tiles, live: (0, tiles[m, s])),
+                pl.BlockSpec(right.shape, lambda s, h, *unused: (0, 0, 0)),
                 thin,
                 wide,
                 wide,
-            ],
-            out_specs=[thin, thin, wide, wide],
+            ]
+            + [pl.BlockSpec(memory_space=pl.ANY)] * len(before),
+            out_specs=[thin, wide, wide],
         ),
         out_shape=[
-            shape(w_in.shape, w_in.dtype),
-            shape(w_out.shape, w_out.dtype),
+            shape(w.shape, w.dtype),
             shape(mom.shape, mom.dtype),
             shape(sec.shape, sec.dtype),
         ],
+        input_output_aliases={7 + i: 1 + i for i in range(len(before))},
         cost_estimate=pl.CostEstimate(
-            flops=2 * toks * mom.size, bytes_accessed=22 * mom.size, transcendentals=mom.size
+            flops=10**10, bytes_accessed=22 * w.size, transcendentals=2 * w.size
         ),
-        name="slot_adam",
-    )(tiles, live, l_in, l_out, r_in, r_out, w_in, w_out, mom, sec)
+        name="slot_part",
+    )(tiles, live, left, right, w, mom, sec, *before)
 
 
 def fused_dims(row_total, col_total, tokens, flat_in, tile_in, owners):
@@ -1024,7 +1110,9 @@
     row_index = lax.axis_index("row")
     owner_rows = owners[:, 0, :]
     ranks = tile_ranks(owner_rows)
-    pick = (owner_rows * slot_cap + ranks).reshape(-1).astype(jnp.int32)
+    owned = (owner_rows == row_index).astype(jnp.int32)
+    slot_of = owner_rows[0] * slot_cap + ranks[0]
+    pick = jnp.concatenate([slot_of, ranks[1] * owned[1], owned[1]]).astype(jnp.int32)
     slot_ids = jnp.arange(slot_cap, dtype=jnp.int32)[None, :, None]
     mine = (owner_rows == row_index)[:, None, :] & (ranks[:, None, :] == slot_ids)
     positions = jnp.arange(tiles, dtype=jnp.int32)
@@ -1034,7 +1122,7 @@
     hidden_out, grad_tokens, grads, act, d_hidden, normed, cot = middle_call(
         dims, pick, tokens, grad_out, gains, flat_in, flat_out, tile_in, tile_out
     )
-    act = act.reshape(all_tok, units)
+    act_rows = act.reshape(rows, all_tok, units)
     d_hidden = d_hidden.reshape(all_tok, units)
 
     def by_row(value):
@@ -1051,28 +1139,30 @@
             placed = lax.dynamic_update_index_in_dim(placed, piece, where, 0)
         return placed
 
-    act_rows = by_row(act)
     d_hidden_rows = by_row(d_hidden)
 
     def spread(grad):
         return lax.all_to_all(grad, both, split_axis=0, concat_axis=0, tiled=True)
 
     pair = spread(grads.reshape(rows * cols, 2 * per, units))
-    new_tile = slot_adam(
+    tile_w_out, tile_m, tile_s = slot_part(
+        1, my_tiles, my_live, cot.reshape(all_tok, width), act_rows, tile_out, tile_moment, tile_second
+    )
+    tile_w_in, tile_m, tile_s = slot_part(
+        0,
         my_tiles,
         my_live,
         normed.reshape(all_tok, width),
-        cot.reshape(all_tok, width),
         d_hidden_rows,
-        act_rows,
         tile_in,
-        tile_out,
         tile_moment,
         tile_second,
+        (tile_m, tile_s),
     )
     new_in, new_out, moment, second = flat_both(
         flat_in, flat_out, pair, flat_moment, flat_second, dims
     )
+    new_tile = (tile_w_in, tile_w_out, tile_m, tile_s)
     return (hidden_out, grad_tokens, new_in, new_out, moment, second, *new_tile)
 
 

time: 371 us -> 331 us (0.89)
  waiting for transfers between devices: 84.8 us -> 57.7 us
  Pallas kernels: 269 us -> 258 us
    ppermute x2 -> x1, waiting for transfers between devices: 84.8 us -> 40.9 us  [by_row(): got.append(lax.ppermute(value, 'row', pairs))]
    all_to_all x1, waiting for transfers between devices: 0.01 us -> 16.9 us  [spread(): return lax.all_to_all(grad, both, split_axis=0, concat_axis=0, tiled=True)]
    pallas_call x1, Pallas kernels: 219 us -> 209 us  [middle_call(): pl.pallas_call(functools.partial(middle_kernel, dims), in_specs=[pl.Block...]
    pallas_call x2 -> x3, Pallas kernels: 50.6 us -> 49.2 us  [the longest x2 32.4 us: slot_part(): pl.pallas_call(functools.partial(slot_kernel_part, m), grid_spec=pltpu.Pr...]
  transfers between devices with their start and end apart: 3 -> 2, of which waited for: 2 -> 2; matrix products, arithmetic and copies ran while one was open for 1% -> 1% of each run, Pallas kernels for 8% -> 10%
where the time goes in v2:
time: 331 us
  Pallas kernels  258 us (78%)
  waiting for transfers between devices  57.7 us (17%)
  starting transfers between devices  6.43 us (2%)
  other arithmetic  6.07 us (2%)
    pallas_call x1, Pallas kernels, middle_call(): pl.pallas_call(functools.partial(middle_kernel, dims), in_specs=[pl.Block...  209 us
    ppermute x1, waiting for transfers between devices, by_row(): got.append(lax.ppermute(value, 'row', pairs))  40.9 us
    pallas_call x2, Pallas kernels, slot_part(): pl.pallas_call(functools.partial(slot_kernel_part, m), grid_spec=pltpu.Pr...  32.4 us
    all_to_all x1, waiting for transfers between devices, spread(): return lax.all_to_all(grad, both, split_axis=0, concat_axis=0, tiled=True)  16.9 us
    pallas_call x1, Pallas kernels, flat_both(): pl.pallas_call(functools.partial(flat_both_kernel, cols, split), grid=(pe...  16.8 us
  transfers between devices with their start and end apart: 2, of which 2 were waited for; matrix products, arithmetic and copies ran while one was open for 1% of the time, Pallas kernels for 10%

profile of v2, /device:TPU:0, one launch (start us, length us, event | category | flops | bytes accessed | tf_op | source)
XLA Modules:
  0.0 330.6 jit_solution(616299191196195309)
XLA Ops:
  0.7 0.7 broadcast_compare_fusion.1
  1.3 1.0 select_reduce_fusion.1
  2.3 0.7 bitcast_add_fusion
  3.0 0.6 pad_add_fusion.pick
  3.6 209.2 %middle.1 = (bf16[16,1024]{1,0:T(8,128)(2,1)}, bf16[16,1024]{1,0:T(8,128)(2,1)}, bf16[32,2,32,1024]{3,2,1,0:T(8,128)(2,1)}, bf16[2,16,2,16,1024]{4,3,2,1,0:T(8,1...) custom-call(s32[12]{0:T(128)} %pad_add_fusion.pick, ...), custom_call_target="tpu_custom_call" | custom-call | flops 12884901888 | bytes 25165824 | tf_op jit(solution)/shard_map/middle/pallas_call | solution.py:904
  212.8 0.0 copy-start
  212.8 0.0 copy-start.3
  212.8 4.7 %all-to-all-start = ((bf16[32,64,1024]{2,1,0:T(8,128)(2,1)}), bf16[32,64,1024]{2,1,0:T(8,128)(2,1)}, u32[]{:S(2)}, u32[]{:S(2)}) async-start(bf16[32,64,1024]{2,1,0:T(8,128)(2,1)} %bitcast.24), calls=%async_computation | async-start | bytes 8388608 | tf_op jit(solution)/shard_map/all_to_all | solution.py:1145
  217.5 0.0 copy-done
  217.5 1.8 collective-permute-start
  219.2 0.0 copy-done.3
  219.3 0.1 fusion.1
  219.4 0.6 convert_element_type.4.live
  220.0 0.7 select_reduce_fusion.tiles
  220.7 16.2 %slot_part.2 = (bf16[1,3,256,2048]{3,2,1,0:T(8,128)(2,1)}, f32[2,1,3,256,2048]{4,3,2,1,0:T(8,128)}, f32[2,1,3,256,2048]{4,3,2,1,0:T(8,128)}) custom-call(s32[2,3]{1,0:T(2,128)} %select_reduce_fusion.tiles, s32[2,3]{1,0:T(2,128)} %convert_element_type.4.live, bf16[512,1024]{1,0:T(8,128)(2,1)} %bitcast.32, bf16[2,512,1024]{2,1,0:T(8,128)(2,1)} %bitcast.31, ...), custom_call_target="tpu_custom_call" | custom-call | flops 10000000000 | bytes 34603008 | tf_op jit(solution)/shard_map/slot_part/pallas_call | solution.py:1042
  236.9 40.9 %collective-permute-done = bf16[512,1024]{1,0:T(8,128)(2,1)S(1)} collective-permute-done((bf16[512,1024]{1,0:T(8,128)(2,1)S(1)}, bf16[512,1024]{1,0:T(8,128)(2,1)S(1)}, u32[]{:S(2)}, u32[]{:S(2)}) %collective-permute-start) | collective-permute-done | bytes 1048608 | tf_op jit(solution)/shard_map/ppermute | solution.py:1132
  277.8 0.2 select_bitcast_fusion.1
  278.0 1.5 pad_maximum_fusion.right
  279.5 16.2 %slot_part.3 = (bf16[1,3,256,2048]{3,2,1,0:T(8,128)(2,1)}, f32[2,1,3,256,2048]{4,3,2,1,0:T(8,128)}, f32[2,1,3,256,2048]{4,3,2,1,0:T(8,128)}) custom-call(s32[2,3]{1,0:T(2,128)} %select_reduce_fusion.tiles, s32[2,3]{1,0:T(2,128)} %convert_element_type.4.live, bf16[512,1024]{1,0:T(8,128)(2,1)} %bitcast.25, ...), custom_call_target="tpu_custom_call", output_to_operand_aliasing={{1}: (7, {}), {2}: (8, {})} | custom-call | flops 10000000000 | bytes 34603008 | tf_op jit(solution)/shard_map/slot_part/pallas_call | solution.py:1042
  295.7 16.9 %all-to-all-done = bf16[32,64,1024]{2,1,0:T(8,128)(2,1)} async-done(((bf16[32,64,1024]{2,1,0:T(8,128)(2,1)}), bf16[32,64,1024]{2,1,0:T(8,128)(2,1)}, u32[]{:S(2)}, u32[]{:S(2)}) %all-to-all-start) | async-done | bytes 4194336 | tf_op jit(solution)/shard_map/all_to_all | solution.py:1145
  312.6 0.0 copy-start.2
  312.6 0.0 copy-start.1
  312.6 16.8 %flat_both.1 = (bf16[512,2048]{1,0:T(8,128)(2,1)}, bf16[512,2048]{1,0:T(8,128)(2,1)}, f32[2,512,2048]{2,1,0:T(8,128)}, f32[2,512,2048]{2,1,0:T(8,128)}) custom-call(bf16[2,16,2,32,1024]{4,3,2,1,0:T(8,128)(2,1)} %bitcast.6.g, bf16[512,2048]{1,0:T(8,128)(2,1)} %w_in.1, bf16[512,2048]{1,0:T(8,128)(2,1)} %w_out.1, f32[2,512,2048]{2,1,0:T(8,128)} %mom.3, ...), custom_call_target="tpu_custom_call" | custom-call | flops 62914560 | bytes 46137344 | tf_op jit(solution)/shard_map/flat_both/pallas_call | solution.py:999
  329.4 0.0 copy-done.2
  329.4 0.6 copy.35
  330.0 0.0 copy-done.1
  330.0 0.6 copy.36
  (5 shorter events, 0.0 us)
Async XLA Ops:
  212.8 4.7 %copy-start = (bf16[16,2,16,1024]{3,2,1,0:T(8,128)(2,1)S(1)}, bf16[16,2,16,1024]{3,2,1,0:T(8,128)(2,1)}, u32[]{:S(2)}) copy-start(bf16[16,2,16,1024]{3,2,1,0:T(8,128)(2,1)} %get-tuple-element.35) | copy-start | bytes 3145732
  212.8 6.5 %copy-start.3 = (s32[2,1,4]{2,1,0:T(1,128)S(1)}, s32[2,1,4]{2,1,0:T(1,128)}, u32[]{:S(2)}) copy-start(s32[2,1,4]{2,1,0:T(1,128)} %param.23) | copy-start | bytes 100
  212.8 99.8 %all-to-all-start = ((bf16[32,64,1024]{2,1,0:T(8,128)(2,1)}), bf16[32,64,1024]{2,1,0:T(8,128)(2,1)}, u32[]{:S(2)}, u32[]{:S(2)}) async-start(bf16[32,64,1024]{2,1,0:T(8,128)(2,1)} %bitcast.24), calls=%async_computation | async-start | bytes 8388608 | tf_op jit(solution)/shard_map/all_to_all | solution.py:1145
  217.5 60.3 %collective-permute-start = (bf16[512,1024]{1,0:T(8,128)(2,1)S(1)}, bf16[512,1024]{1,0:T(8,128)(2,1)S(1)}, u32[]{:S(2)}, u32[]{:S(2)}) collective-permute-start(bf16[512,1024]{1,0:T(8,128)(2,1)S(1)} %bitcast.26), channel_id=1, source_target_pairs={{0,16},{16,0},{1,17},{17,1},{2,18},{18,2},{3,19},{19,3},{4,20},{20... | collective-permute-start | bytes 3145736 | tf_op jit(solution)/shard_map/ppermute | solution.py:1132
  312.6 16.8 %copy-start.2 = (bf16[16,1024]{1,0:T(8,128)(2,1)S(1)}, bf16[16,1024]{1,0:T(8,128)(2,1)}, u32[]{:S(2)}) copy-start(bf16[16,1024]{1,0:T(8,128)(2,1)} %get-tuple-element.56) | copy-start | bytes 98308
  312.6 17.4 %copy-start.1 = (bf16[16,1024]{1,0:T(8,128)(2,1)S(1)}, bf16[16,1024]{1,0:T(8,128)(2,1)}, u32[]{:S(2)}) copy-start(bf16[16,1024]{1,0:T(8,128)(2,1)} %get-tuple-element.57) | copy-start | bytes 98308

commit v3 on v2

--- a/solution.py
+++ b/solution.py
@@ -450,6 +450,31 @@
         sent.extend(out)
         return out
 
+    def ag_y(g, n):
+        out = []
+        for dr in range(1, rows):
+            here = g.at[r, :, x, core]
+            sems = ag_send.at[n, zs + dr - 1], ag_recv.at[n, zs + dr - 1]
+            out.append(remote(here, here, *sems, lax.rem(r + dr, rows), col_of(z, x, core)))
+        for cp in out:
+            cp.start()
+        sent.extend(out)
+        return out
+
+    def ag_x(g, n):
+        out = []
+        for dx in range(1, xs):
+            here = g.at[:, :, x, core]
+            j = zs + rows - 2 + dx
+            xt = lax.rem(x + dx, xs)
+            out.append(
+                remote(here, here, ag_send.at[n, j], ag_recv.at[n, j], r, col_of(z, xt, core))
+            )
+        for cp in out:
+            cp.start()
+        sent.extend(out)
+        return out
+
     def ag_core(g, n):
         here = g.at[:, :, :, core]
         cp = remote(here, here, ag_send.at[n, 0], ag_recv.at[n, 0], r, col_of(z, x, 1 - core))
@@ -643,18 +668,22 @@
     loads[0].wait()
     permute(0)
     arrived(one_z)
-    one_xy = ag_xy(g1, 0)
+    one_y = ag_y(g1, 0)
     arrived(cot_z)
-    cot_xy = ag_xy(gc, 1)
+    cot_y = ag_y(gc, 1)
     a2a_start(0, 1)
     slots_start(1, 2 * slot_cap)
     loads[1].wait()
     permute(1)
     a2a_start(1, 1)
-    arrived(one_xy)
+    arrived(cot_y)
+    cot_x = ag_x(gc, 1)
+    arrived(one_y)
+    one_x = ag_x(g1, 0)
+    arrived(cot_x)
+    cot_c = ag_core(gc, 1)
+    arrived(one_x)
     one_c = ag_core(g1, 0)
-    arrived(cot_xy)
-    cot_c = ag_core(gc, 1)
 
     arrived(one_c)
     arrived(cot_c)

time: 331 us -> 325 us (0.982)
  Pallas kernels: 258 us -> 252 us
    pallas_call x1, Pallas kernels: 209 us -> 203 us  [middle_call(): pl.pallas_call(functools.partial(middle_kernel, dims), in_specs=[pl.Block...]
where the time goes in v3:
time: 325 us; the launch traced here: 324 us
  Pallas kernels  252 us (78%)
  waiting for transfers between devices  57.7 us (18%)
  starting transfers between devices  6.46 us (2%)
  other arithmetic  6.07 us (2%)
    pallas_call x1, Pallas kernels, middle_call(): pl.pallas_call(functools.partial(middle_kernel, dims), in_specs=[pl.Block...  203 us
    ppermute x1, waiting for transfers between devices, by_row(): got.append(lax.ppermute(value, 'row', pairs))  40.9 us
    pallas_call x2, Pallas kernels, slot_part(): pl.pallas_call(functools.partial(slot_kernel_part, m), grid_spec=pltpu.Pr...  32.4 us
    all_to_all x1, waiting for transfers between devices, spread(): return lax.all_to_all(grad, both, split_axis=0, concat_axis=0, tiled=True)  16.9 us
    pallas_call x1, Pallas kernels, flat_both(): pl.pallas_call(functools.partial(flat_both_kernel, cols, split), grid=(pe...  16.8 us
  transfers between devices with their start and end apart: 2, of which 2 were waited for; matrix products, arithmetic and copies ran while one was open for 1% of the time, Pallas kernels for 10%

profile of v3, /device:TPU:0, one launch (start us, length us, event | category | flops | bytes accessed | tf_op | source)
XLA Modules:
  0.0 324.3 jit_solution(12489799468278564234)
XLA Ops:
  0.7 0.7 broadcast_compare_fusion.1
  1.3 1.0 select_reduce_fusion.1
  2.3 0.7 bitcast_add_fusion
  3.0 0.6 pad_add_fusion.pick
  3.6 202.8 %middle.1 = (bf16[16,1024]{1,0:T(8,128)(2,1)}, bf16[16,1024]{1,0:T(8,128)(2,1)}, bf16[32,2,32,1024]{3,2,1,0:T(8,128)(2,1)}, bf16[2,16,2,16,1024]{4,3,2,1,0:T(8,1...) custom-call(s32[12]{0:T(128)} %pad_add_fusion.pick, ...), custom_call_target="tpu_custom_call" | custom-call | flops 12884901888 | bytes 25165824 | tf_op jit(solution)/shard_map/middle/pallas_call | solution.py:933
  206.4 0.0 copy-start
  206.5 0.0 copy-start.3
  206.5 4.7 %all-to-all-start = ((bf16[32,64,1024]{2,1,0:T(8,128)(2,1)}), bf16[32,64,1024]{2,1,0:T(8,128)(2,1)}, u32[]{:S(2)}, u32[]{:S(2)}) async-start(bf16[32,64,1024]{2,1,0:T(8,128)(2,1)} %bitcast.24), calls=%async_computation | async-start | bytes 8388608 | tf_op jit(solution)/shard_map/all_to_all | solution.py:1174
  211.2 0.0 copy-done
  211.2 1.8 collective-permute-start
  212.9 0.0 copy-done.3
  213.0 0.1 fusion.1
  213.1 0.6 convert_element_type.4.live
  213.7 0.7 select_reduce_fusion.tiles
  214.4 16.2 %slot_part.2 = (bf16[1,3,256,2048]{3,2,1,0:T(8,128)(2,1)}, f32[2,1,3,256,2048]{4,3,2,1,0:T(8,128)}, f32[2,1,3,256,2048]{4,3,2,1,0:T(8,128)}) custom-call(s32[2,3]{1,0:T(2,128)} %select_reduce_fusion.tiles, s32[2,3]{1,0:T(2,128)} %convert_element_type.4.live, bf16[512,1024]{1,0:T(8,128)(2,1)} %bitcast.32, bf16[2,512,1024]{2,1,0:T(8,128)(2,1)} %bitcast.31, ...), custom_call_target="tpu_custom_call" | custom-call | flops 10000000000 | bytes 34603008 | tf_op jit(solution)/shard_map/slot_part/pallas_call | solution.py:1071
  230.6 40.9 %collective-permute-done = bf16[512,1024]{1,0:T(8,128)(2,1)S(1)} collective-permute-done((bf16[512,1024]{1,0:T(8,128)(2,1)S(1)}, bf16[512,1024]{1,0:T(8,128)(2,1)S(1)}, u32[]{:S(2)}, u32[]{:S(2)}) %collective-permute-start) | collective-permute-done | bytes 1048608 | tf_op jit(solution)/shard_map/ppermute | solution.py:1161
  271.5 0.2 select_bitcast_fusion.1
  271.7 1.5 pad_maximum_fusion.right
  273.2 16.2 %slot_part.3 = (bf16[1,3,256,2048]{3,2,1,0:T(8,128)(2,1)}, f32[2,1,3,256,2048]{4,3,2,1,0:T(8,128)}, f32[2,1,3,256,2048]{4,3,2,1,0:T(8,128)}) custom-call(s32[2,3]{1,0:T(2,128)} %select_reduce_fusion.tiles, s32[2,3]{1,0:T(2,128)} %convert_element_type.4.live, bf16[512,1024]{1,0:T(8,128)(2,1)} %bitcast.25, ...), custom_call_target="tpu_custom_call", output_to_operand_aliasing={{1}: (7, {}), {2}: (8, {})} | custom-call | flops 10000000000 | bytes 34603008 | tf_op jit(solution)/shard_map/slot_part/pallas_call | solution.py:1071
  289.4 16.9 %all-to-all-done = bf16[32,64,1024]{2,1,0:T(8,128)(2,1)} async-done(((bf16[32,64,1024]{2,1,0:T(8,128)(2,1)}), bf16[32,64,1024]{2,1,0:T(8,128)(2,1)}, u32[]{:S(2)}, u32[]{:S(2)}) %all-to-all-start) | async-done | bytes 4194336 | tf_op jit(solution)/shard_map/all_to_all | solution.py:1174
  306.3 0.0 copy-start.2
  306.3 0.0 copy-start.1
  306.3 16.8 %flat_both.1 = (bf16[512,2048]{1,0:T(8,128)(2,1)}, bf16[512,2048]{1,0:T(8,128)(2,1)}, f32[2,512,2048]{2,1,0:T(8,128)}, f32[2,512,2048]{2,1,0:T(8,128)}) custom-call(bf16[2,16,2,32,1024]{4,3,2,1,0:T(8,128)(2,1)} %bitcast.6.g, bf16[512,2048]{1,0:T(8,128)(2,1)} %w_in.1, bf16[512,2048]{1,0:T(8,128)(2,1)} %w_out.1, f32[2,512,2048]{2,1,0:T(8,128)} %mom.3, ...), custom_call_target="tpu_custom_call" | custom-call | flops 62914560 | bytes 46137344 | tf_op jit(solution)/shard_map/flat_both/pallas_call | solution.py:1028
  323.1 0.0 copy-done.2
  323.1 0.6 copy.35
  323.7 0.0 copy-done.1
  323.7 0.6 copy.36
  (5 shorter events, 0.0 us)
Async XLA Ops:
  206.4 4.7 %copy-start = (bf16[16,2,16,1024]{3,2,1,0:T(8,128)(2,1)S(1)}, bf16[16,2,16,1024]{3,2,1,0:T(8,128)(2,1)}, u32[]{:S(2)}) copy-start(bf16[16,2,16,1024]{3,2,1,0:T(8,128)(2,1)} %get-tuple-element.35) | copy-start | bytes 3145732
  206.5 6.5 %copy-start.3 = (s32[2,1,4]{2,1,0:T(1,128)S(1)}, s32[2,1,4]{2,1,0:T(1,128)}, u32[]{:S(2)}) copy-start(s32[2,1,4]{2,1,0:T(1,128)} %param.23) | copy-start | bytes 100
  206.5 99.8 %all-to-all-start = ((bf16[32,64,1024]{2,1,0:T(8,128)(2,1)}), bf16[32,64,1024]{2,1,0:T(8,128)(2,1)}, u32[]{:S(2)}, u32[]{:S(2)}) async-start(bf16[32,64,1024]{2,1,0:T(8,128)(2,1)} %bitcast.24), calls=%async_computation | async-start | bytes 8388608 | tf_op jit(solution)/shard_map/all_to_all | solution.py:1174
  211.2 60.3 %collective-permute-start = (bf16[512,1024]{1,0:T(8,128)(2,1)S(1)}, bf16[512,1024]{1,0:T(8,128)(2,1)S(1)}, u32[]{:S(2)}, u32[]{:S(2)}) collective-permute-start(bf16[512,1024]{1,0:T(8,128)(2,1)S(1)} %bitcast.26), channel_id=1, source_target_pairs={{0,16},{16,0},{1,17},{17,1},{2,18},{18,2},{3,19},{19,3},{4,20},{20... | collective-permute-start | bytes 3145736 | tf_op jit(solution)/shard_map/ppermute | solution.py:1161
  306.3 16.8 %copy-start.2 = (bf16[16,1024]{1,0:T(8,128)(2,1)S(1)}, bf16[16,1024]{1,0:T(8,128)(2,1)}, u32[]{:S(2)}) copy-start(bf16[16,1024]{1,0:T(8,128)(2,1)} %get-tuple-element.56) | copy-start | bytes 98308
  306.3 17.4 %copy-start.1 = (bf16[16,1024]{1,0:T(8,128)(2,1)S(1)}, bf16[16,1024]{1,0:T(8,128)(2,1)}, u32[]{:S(2)}) copy-start(bf16[16,1024]{1,0:T(8,128)(2,1)} %get-tuple-element.57) | copy-start | bytes 98308
